TPU v7x, 1024 devices: a whole 8x8x8 slice. The times are simulated.
1024 devices in a mesh: curve: 16 (over y, core), group: 64 (over z, x).
Axes of the slice: x: 8, y: 8, z: 8, core: 2. Of those that a mesh axis runs over, the one named last changes fastest.
Arguments:
- right_side: float32 [125, 524288], P(None, ('curve', 'group')), may hold values from -6 to 6, as said below
- conductivity: float32 [524288], P(('curve', 'group')), may hold values from 0.3 to 3
- destination: int32 [524288], P(('curve', 'group')), may hold values from 0 to 524287, as said below
- neighbour: int32 [6, 524288], P(None, ('curve', 'group')), may hold values from -1 to 1023, as said below
- orientation: int32 [6, 524288], P(None, ('curve', 'group')), may hold values from 0 to 3, as said below
- send_list: int32 [2, 262144], P(None, ('curve', 'group')), may hold values from 0 to 511, as said below
Outputs:
- solution: float32 [125, 524288], P(None, ('curve', 'group'))
- residual: float32 [125, 524288], P(None, ('curve', 'group'))
Inputs may be any that keep to these rules, and one draw needn't show every extreme that they name: `right_side`: custom normal-like values. `destination`: A permutation of all cells. Devices are ordered along the curve with curve slowest; every cell's new device is its old device or the one just before or after it. From each device at most 64 cells go to the next device and exactly as many come back from it; 64 is reached at some pair of neighbouring devices in every draw. `neighbour`: values below 512 are local cells of the same device. Only face 0 may name a slot from 512 to 512 + 256 - 1 (filled by the previous device from its send_list row 1), only face 1 a slot from 768 up (filled by the next device from its send_list row 0). Faces are paired: the cell across face f sees this cell across face f xor 1. -1 only at the domain boundary; the first device has no partner across its face 0 slots and the last none across face 1 slots. `orientation`: both sides of a shared face carry the same code; ignored where neighbour is -1. `send_list`: per device 256 distinct local cells in each row.
All inputs are finite; a program needn't handle non-finite values.
Results may differ from a plain program's by a relative error of at most 0.00015.
Values sent between devices are 32-bit elements; how exact they have to be, the bound alone decides.
A program may use at most 32 MiB of HBM per device.

v0:
```python
import functools

import jax
import jax.numpy as jnp
from jax import lax
from jax.sharding import Mesh
from jax.sharding import PartitionSpec as P

NODES = 5
ITERS = 2
BLOCK = 125
MOVE = 64
CURVE_GROUP = ("curve_0", "curve_1", "group_0", "group_1")
CURVE = ("curve_0", "curve_1")
GROUP = ("group_0", "group_1")


PENALTY = 80.0
HIGHEST = lax.Precision.HIGHEST
GAUSS_POINTS = (-0.906179845938664, -0.5384693101056831, 0.0, 0.5384693101056831, 0.906179845938664)
GAUSS_WEIGHTS = (
    0.2369268850561891,
    0.4786286704993665,
    0.5688888888888889,
    0.4786286704993665,
    0.2369268850561891,
)


def with_halo(shard, sides, width):
    edges = {}
    for axis, dim in sides:
        size, length = (lax.axis_size(axis), shard.shape[dim])
        up = [(i, (i + 1) % size) for i in range(size - 1)]
        last = lax.slice_in_dim(shard, length - width, length, axis=dim)
        initial = lax.slice_in_dim(shard, 0, width, axis=dim)
        edges[dim] = (
            lax.ppermute(last, axis, up),
            lax.ppermute(initial, axis, [(b, a) for a, b in up]),
        )
    done = []
    for _, dim in sides:
        low, high = edges[dim]
        around = [(width, width) if d in done else (0, 0) for d in range(shard.ndim)]
        shard = jnp.concatenate([jnp.pad(low, around), shard, jnp.pad(high, around)], axis=dim)
        done.append(dim)
    return shard


def by_axis(shard, axes):
    return functools.reduce(lax.psum, axes, shard)


def lagrange_value(points, position, location):
    product_value = 1.0
    for other_id in range(len(points)):
        if other_id != position:
            product_value = (
                product_value
                * (location - points[other_id])
                / (points[position] - points[other_id])
            )
    return product_value


def lagrange_slope(points, position, location):
    slope_sum = 0.0
    for skipped in range(len(points)):
        if skipped == position:
            continue
        addend = 1.0 / (points[position] - points[skipped])
        for other_id in range(len(points)):
            if other_id != position and other_id != skipped:
                addend = (
                    addend * (location - points[other_id]) / (points[position] - points[other_id])
                )
        slope_sum = slope_sum + addend
    return slope_sum


def basis_tables():
    points = [0.5 * (value + 1.0) for value in GAUSS_POINTS]
    weights = [0.5 * value for value in GAUSS_WEIGHTS]
    count = len(points)
    slopes = [
        [lagrange_slope(points, column, points[row_id]) for column in range(count)]
        for row_id in range(count)
    ]
    start_value = [lagrange_value(points, column, 0.0) for column in range(count)]
    end_value = [lagrange_value(points, column, 1.0) for column in range(count)]
    start_slope = [-lagrange_slope(points, column, 0.0) for column in range(count)]
    end_slope = [lagrange_slope(points, column, 1.0) for column in range(count)]
    listed = (weights, slopes, start_value, end_value, start_slope, end_slope)
    return tuple((jnp.asarray(table, jnp.float32) for table in listed))


def face_vectors(face_id, tables):
    if face_id % 2:
        return (tables[3], tables[5])
    return (tables[2], tables[4])


def along_axis(matrix, axis_id):
    eye_five = jnp.eye(NODES, dtype=jnp.float32)
    eye_plane = jnp.eye(NODES * NODES, dtype=jnp.float32)
    if axis_id == 0:
        return jnp.kron(matrix, eye_plane)
    if axis_id == 1:
        return jnp.kron(eye_five, jnp.kron(matrix, eye_five))
    return jnp.kron(eye_plane, matrix)


def operator_tables(tables):
    weights, slopes = (tables[0], tables[1])
    grad_matrix = jnp.concatenate([along_axis(slopes, axis_id) for axis_id in range(3)], 0)
    cell_weight = jnp.kron(weights, jnp.kron(weights, weights))
    value_rows = []
    normal_rows = []
    for face_id in range(6):
        trace_vec, normal_vec = face_vectors(face_id, tables)
        value_rows.append(along_axis(trace_vec[None, :], face_id // 2))
        normal_rows.append(along_axis(normal_vec[None, :], face_id // 2))
    trace_matrix = jnp.concatenate(value_rows + normal_rows, 0)
    face_weight = jnp.kron(weights, weights)[:, None]
    row_ids = jnp.arange(NODES * NODES, dtype=jnp.int32)
    flip_first = (NODES - 1 - row_ids // NODES) * NODES + row_ids % NODES
    flip_second = row_ids // NODES * NODES + NODES - 1 - row_ids % NODES
    return (grad_matrix, cell_weight, trace_matrix, face_weight, flip_first, flip_second)


def product(matrix, field):
    return jnp.dot(matrix, field, precision=HIGHEST, preferred_element_type=jnp.float32)


def operate(field, conduct, neighbour, orientation, send_list, ops):
    grad_matrix, cell_weight, trace_matrix, face_weight, flip_first, flip_second = ops
    face_size = NODES * NODES
    face_all = product(trace_matrix, field)
    values = face_all[: 6 * face_size]
    fluxes = conduct[None] * face_all[6 * face_size :]

    def pack_face(face_id, chosen):
        packed_rows = jnp.concatenate(
            [
                values[face_id * face_size : (face_id + 1) * face_size],
                fluxes[face_id * face_size : (face_id + 1) * face_size],
                conduct[None],
            ],
            0,
        )
        return packed_rows[:, chosen]

    stacked = jnp.stack([pack_face(0, send_list[0]), pack_face(1, send_list[1])])
    received = with_halo(stacked, ((CURVE_GROUP, 0),), 1)
    left_value = received[0][:face_size]
    left_flux = received[0][face_size : 2 * face_size]
    left_conduct = received[0][2 * face_size]
    right_value = received[3][:face_size]
    right_flux = received[3][face_size : 2 * face_size]
    right_conduct = received[3][2 * face_size]
    grads = product(grad_matrix, field)
    weight_three = jnp.tile(cell_weight, 3)[:, None]
    result = cell_weight[:, None] * field + product(
        grad_matrix.T, weight_three * conduct[None] * grads
    )
    value_terms = []
    normal_terms = []
    for face_id in range(6):
        own_value = values[face_id * face_size : (face_id + 1) * face_size]
        own_flux = fluxes[face_id * face_size : (face_id + 1) * face_size]
        other_id = face_id ^ 1
        other_value = values[other_id * face_size : (other_id + 1) * face_size]
        other_flux = fluxes[other_id * face_size : (other_id + 1) * face_size]
        other_conduct = conduct
        if face_id < 2:
            other_value = jnp.concatenate([other_value, left_value, right_value], 1)
            other_flux = jnp.concatenate([other_flux, left_flux, right_flux], 1)
            other_conduct = jnp.concatenate([conduct, left_conduct, right_conduct])
        partner = neighbour[face_id]
        safe_idx = jnp.where(partner < 0, 0, partner)
        near_value = other_value[:, safe_idx]
        near_flux = other_flux[:, safe_idx]
        near_conduct = other_conduct[safe_idx]
        code = orientation[face_id]
        first_bit = (code % 2 == 1)[None]
        second_bit = (code // 2 == 1)[None]
        near_value = jnp.where(first_bit, near_value[flip_first], near_value)
        near_value = jnp.where(second_bit, near_value[flip_second], near_value)
        near_flux = jnp.where(first_bit, near_flux[flip_first], near_flux)
        near_flux = jnp.where(second_bit, near_flux[flip_second], near_flux)
        outside = (partner < 0)[None]
        near_value = jnp.where(outside, -own_value, near_value)
        near_flux = jnp.where(outside, -own_flux, near_flux)
        near_conduct = jnp.where(partner < 0, conduct, near_conduct)
        penalty = PENALTY * jnp.maximum(conduct, near_conduct)[None]
        trace_jump = own_value - near_value
        mean_flux = 0.5 * (own_flux - near_flux)
        value_terms.append(face_weight * (penalty * trace_jump - mean_flux))
        normal_terms.append(face_weight * (-0.5 * conduct[None] * trace_jump))
    coefficients = jnp.concatenate(value_terms + normal_terms, 0)
    return result + product(trace_matrix.T, coefficients)


def migrate(right_side, conductivity, destination):
    cell_count = destination.shape[0]
    my_rank = lax.axis_index(CURVE) * lax.axis_size(GROUP) + lax.axis_index(GROUP)
    target = destination // cell_count - my_rank
    new_slot = destination % cell_count
    payload = jnp.concatenate([right_side, conductivity[None]], 0)
    stay_slot = jnp.where(target == 0, new_slot, cell_count)
    arrived = (
        jnp.zeros((BLOCK + 1, cell_count), jnp.float32).at[:, stay_slot].set(payload, mode="drop")
    )
    tagged = jnp.concatenate([payload, (new_slot + 1).astype(jnp.float32)[None]], 0)

    def pack_moving(leaving):
        packed_slot = jnp.cumsum(leaving.astype(jnp.int32)) - 1
        packed_slot = jnp.where(leaving, packed_slot, MOVE)
        return jnp.zeros((BLOCK + 2, MOVE), jnp.float32).at[:, packed_slot].set(tagged, mode="drop")

    stacked = jnp.stack([pack_moving(target == -1), pack_moving(target == 1)])
    received = with_halo(stacked, ((CURVE_GROUP, 0),), 1)
    for record in (received[0], received[3]):
        placing = record[BLOCK + 1].astype(jnp.int32) - 1
        placing = jnp.where(placing < 0, cell_count, placing)
        arrived = arrived.at[:, placing].set(record[: BLOCK + 1], mode="drop")
    return (arrived[:BLOCK], arrived[BLOCK])


def two_products(residual, image):
    return (
        by_axis(jnp.sum(residual * residual), CURVE_GROUP),
        by_axis(jnp.sum(residual * image), CURVE_GROUP),
    )


def body(right_side, conductivity, destination, neighbour, orientation, send_list):
    tables = basis_tables()
    ops = operator_tables(tables)
    source, conduct = migrate(right_side, conductivity, destination)

    def apply_operator(field):
        return operate(field, conduct, neighbour, orientation, send_list, ops)

    solution = jnp.zeros_like(source)
    residual = source
    image = apply_operator(residual)
    norm_now, inner = two_products(residual, image)
    step_size = norm_now / inner
    direction, along = (residual, image)
    for step in range(ITERS):
        solution = solution + step_size * direction
        residual = residual - step_size * along
        if step + 1 < ITERS:
            image = apply_operator(residual)
            norm_next, inner = two_products(residual, image)
            beta_ratio = norm_next / norm_now
            step_size = norm_next / (inner - beta_ratio * norm_next / step_size)
            direction = residual + beta_ratio * direction
            along = image + beta_ratio * along
            norm_now = norm_next
    return (solution, residual)


def solution(mesh):
    split = Mesh(mesh.devices.reshape(8, 2, 8, 8), ("curve_0", "curve_1", "group_0", "group_1"))
    in_specs = (
        P(None, CURVE_GROUP),
        P(CURVE_GROUP),
        P(CURVE_GROUP),
        P(None, CURVE_GROUP),
        P(None, CURVE_GROUP),
        P(None, CURVE_GROUP),
    )
    out_specs = (P(None, CURVE_GROUP), P(None, CURVE_GROUP))
    return jax.shard_map(body, mesh=split, in_specs=in_specs, out_specs=out_specs, check_vma=False)
```

profile of v0, /device:TPU:16, one launch (start us, length us, event | category | flops | bytes accessed | tf_op | source)
XLA Modules:
  0.0 381.3 jit_solution(6634528102876500395)
XLA Ops:
  2.4 1.3 add_convert_fusion
  4.9 2.3 scatter_custom_fusion.1
  7.2 3.4 collective-permute-start
  10.6 2.3 scatter_custom_fusion.3
  12.8 17.3 %collective-permute-start.1 = (f32[1,127,64]{1,2,0:T(8,128)}, f32[1,127,64]{1,2,0:T(8,128)}, u32[]{:S(2)}, u32[]{:S(2)}) collective-permute-start(f32[1,127,64]{1,2,0:T(8,128)} %bitcast.12), channel_id=1, source_target_pairs={{1,0},{2,1},{3,2},{4,3},{5,4},{6,5},{7,6},{8,7},{9,8},{10,9},{11,1... | collective-permute-start | bytes 97544 | tf_op jit(solution)/shard_map/ppermute | solution.py:39
  52.4 1.3 pad_clamp_fusion.6
  55.4 1.8 compare_reduce_fusion.1
  57.2 1.4 broadcast_multiply_fusion.8
  61.0 1.2 mul.1213
  63.8 2.2 scatter_custom_fusion
  66.0 5.9 %concatenate.66 = f32[300,125]{1,0:T(8,128)S(1)} concatenate(f32[25,125]{1,0:T(8,128)} %get-tuple-element.183, f32[25,125]{1,0:T(8,128)} %get-tuple-element.184, f32[25,125]{1,0:T(8,128)S(1)} %mul.1239, f32[25,125]{1,0:T(8,128)S(1)} %mul.1246, f32[25,125]{1,0:T(8,128)} %get-tuple-element.134, f32[25,125]{1,0:T(8,128)} %get-tuple-element.133, f32[25,125]{1,0:T(8,128)} %get-tuple-element.185, ...), dimensions={0} | concatenate | bytes 300000 | tf_op jit(solution)/shard_map/concatenate | solution.py:123
  78.4 3.4 collective-permute-start.3
  83.5 2.8 collective-permute-start.2
  95.6 4.6 %gather_fusion.37 = f32[512]{0:T(512)} fusion(f32[512]{0:T(512)S(1)} %bitcast.179, s32[1024]{0:T(1024)S(1)} %copy-done.41), kind=kCustom, calls=%fused_computation.37 | custom fusion | bytes 6144 | tf_op jit(solution)/shard_map/gather | solution.py:183
  100.2 4.7 %gather_fusion.16 = f32[512]{0:T(512)} fusion(f32[512]{0:T(512)S(1)} %bitcast.180, s32[1024]{0:T(1024)S(1)} %copy-done.32), kind=kCustom, calls=%fused_computation.16 | custom fusion | bytes 6144 | tf_op jit(solution)/shard_map/gather | solution.py:183
  104.9 4.7 %gather_fusion.30 = f32[512]{0:T(512)} fusion(f32[512]{0:T(512)S(1)} %bitcast.181, s32[1024]{0:T(1024)S(1)} %copy-done.35), kind=kCustom, calls=%fused_computation.30 | custom fusion | bytes 6144 | tf_op jit(solution)/shard_map/gather | solution.py:183
  109.6 4.6 %gather_fusion.23 = f32[512]{0:T(512)} fusion(f32[512]{0:T(512)S(1)} %bitcast.182, s32[1024]{0:T(1024)S(1)} %copy-done.38), kind=kCustom, calls=%fused_computation.23 | custom fusion | bytes 6144 | tf_op jit(solution)/shard_map/gather | solution.py:183
  116.7 1.2 gather_fusion.28
  120.4 1.2 gather_fusion.35
  122.9 3.4 gather_fusion.9
  126.3 3.4 gather_fusion.2
  130.0 1.6 gather_fusion.10
  134.4 1.6 gather_fusion.13
  144.4 1.6 gather_fusion.3
  148.9 1.6 gather_fusion.6
  152.9 1.2 gather_fusion.8
  154.7 1.2 gather_fusion.15
  160.7 1.5 multiply_multiply_fusion.7
  165.0 3.6 concatenate.74
  168.6 1.3 multiply_reduce_fusion.2
  169.9 18.3 %all-reduce.5 = (f32[]{:T(128)}, f32[]{:T(128)}) all-reduce(f32[]{:T(128)} %get-tuple-element.5, f32[]{:T(128)} %get-tuple-element.4), channel_id=1, replica_groups=mesh['curve_0'=8,'curve_1'=2,'group_0'=8,'group_1'=8] {'curve_0'}, use_global_device_ids=true, to_apply=%region_10.11 | all-reduce | flops 2 | bytes 16 | tf_op jit(solution)/shard_map/psum | solution.py:51
  188.2 3.1 all-reduce.7
  191.3 16.4 %all-reduce.3 = (f32[]{:T(128)}, f32[]{:T(128)}) all-reduce(f32[]{:T(128)} %get-tuple-element.38, f32[]{:T(128)} %get-tuple-element.39), channel_id=1, replica_groups=mesh['curve_0'=8,'curve_1'=2,'group_0'=8,'group_1'=8] {'group_0'}, use_global_device_ids=true, to_apply=%region_12.13 | all-reduce | flops 2 | bytes 16 | tf_op jit(solution)/shard_map/psum | solution.py:51
  207.7 18.9 %all-reduce.1 = (f32[]{:T(128)}, f32[]{:T(128)}) all-reduce(f32[]{:T(128)} %get-tuple-element.30, f32[]{:T(128)} %get-tuple-element.31), channel_id=1, replica_groups=mesh['curve_0'=8,'curve_1'=2,'group_0'=8,'group_1'=8] {'group_1'}, use_global_device_ids=true, to_apply=%region_13.14 | all-reduce | flops 2 | bytes 16 | tf_op jit(solution)/shard_map/psum | solution.py:51
  232.1 1.2 gather_fusion.79
  234.7 1.2 gather_fusion.82
  237.7 1.9 collective-permute-start.5
  241.3 3.9 %collective-permute-start.4 = (f32[1,51,256]{2,1,0:T(8,128)}, f32[1,51,256]{2,1,0:T(8,128)}, u32[]{:S(2)}, u32[]{:S(2)}) collective-permute-start(f32[1,51,256]{2,1,0:T(8,128)} %bitcast.71), channel_id=1, source_target_pairs={{0,1},{1,2},{2,3},{3,4},{4,5},{5,6},{6,7},{7,8},{8,9},{9,10},{10,1... | collective-permute-start | bytes 156680 | tf_op jit(solution)/shard_map/ppermute | solution.py:38
  247.4 1.2 gather_fusion.67
  254.4 1.6 gather_fusion.75
  257.1 1.2 gather_fusion.76
  258.3 1.2 gather_fusion.71
  260.9 1.6 gather_fusion.63
  263.6 1.2 gather_fusion.64
  266.3 3.4 gather_fusion.53
  269.7 3.4 gather_fusion.46
  276.6 1.6 gather_fusion.47
  280.8 1.6 gather_fusion.50
  286.8 1.6 gather_fusion.54
  289.5 1.2 gather_fusion.55
  291.8 1.6 gather_fusion.57
  296.7 1.4 multiply_multiply_fusion
  298.3 1.6 gather_fusion.72
  303.5 1.2 gather_fusion.59
  305.7 1.6 gather_fusion.60
  309.9 1.2 gather_fusion.65
  312.4 1.4 multiply_multiply_fusion.1
  313.9 1.6 subtract_multiply_fusion.2
  317.3 5.2 %concatenate.82 = f32[300,512]{1,0:T(8,128)S(1)} concatenate(f32[25,512]{1,0:T(8,128)S(1)} %get-tuple-element.46, f32[25,512]{1,0:T(8,128)S(1)} %get-tuple-element.48, f32[25,512]{1,0:T(8,128)} %get-tuple-element.50, f32[25,512]{1,0:T(8,128)} %get-tuple-element.49, f32[25,512]{1,0:T(8,128)S(1)} %get-tuple-element.47, f32[25,512]{1,0:T(8,128)S(1)} %get-tuple-element.45, ...), dimensions={0} | concatenate | bytes 1228800 | tf_op jit(solution)/shard_map/concatenate | solution.py:200
  322.6 1.3 multiply_reduce_fusion
  323.9 17.4 %all-reduce.4 = (f32[]{:T(128)}, f32[]{:T(128)}) all-reduce(f32[]{:T(128)} %get-tuple-element.3, f32[]{:T(128)} %get-tuple-element.2), channel_id=1, replica_groups=mesh['curve_0'=8,'curve_1'=2,'group_0'=8,'group_1'=8] {'curve_0'}, use_global_device_ids=true, to_apply=%region_20.21 | all-reduce | flops 2 | bytes 16 | tf_op jit(solution)/shard_map/psum | solution.py:51
  341.2 3.1 all-reduce.6
  344.3 14.8 %all-reduce.2 = (f32[]{:T(128)}, f32[]{:T(128)}) all-reduce(f32[]{:T(128)} %get-tuple-element.36, f32[]{:T(128)} %get-tuple-element.37), channel_id=1, replica_groups=mesh['curve_0'=8,'curve_1'=2,'group_0'=8,'group_1'=8] {'group_0'}, use_global_device_ids=true, to_apply=%region_22.23 | all-reduce | flops 2 | bytes 16 | tf_op jit(solution)/shard_map/psum | solution.py:51
  359.1 16.7 %all-reduce = (f32[]{:T(128)}, f32[]{:T(128)}) all-reduce(f32[]{:T(128)} %get-tuple-element.28, f32[]{:T(128)} %get-tuple-element.29), channel_id=1, replica_groups=mesh['curve_0'=8,'curve_1'=2,'group_0'=8,'group_1'=8] {'group_1'}, use_global_device_ids=true, to_apply=%region_23.24 | all-reduce | flops 2 | bytes 16 | tf_op jit(solution)/shard_map/psum | solution.py:51
  (392 shorter events, 126.7 us)
Async XLA Ops:
  0.6 31.7 %copy-start.43 = (f32[5,5]{1,0:T(8,128)S(1)}, f32[5,5]{1,0:T(8,128)}, u32[]{:S(2)}) copy-start(f32[5,5]{1,0:T(8,128)} %constant.231.clone) | copy-start | bytes 304
  3.7 29.8 %copy-start.68 = (f32[5]{0:T(128)S(1)}, f32[5]{0:T(128)}, u32[]{:S(2)}) copy-start(f32[5]{0:T(128)} %constant.230.clone) | copy-start | bytes 64
  7.2 64.7 %collective-permute-start = (f32[1,127,64]{1,2,0:T(8,128)}, f32[1,127,64]{1,2,0:T(8,128)}, u32[]{:S(2)}, u32[]{:S(2)}) collective-permute-start(f32[1,127,64]{1,2,0:T(8,128)} %bitcast.6), channel_id=1, source_target_pairs={{0,1},{1,2},{2,3},{3,4},{4,5},{5,6},{6,7},{7,8},{8,9},{9,10},{10,1... | collective-permute-start | bytes 97544 | tf_op jit(solution)/shard_map/ppermute | solution.py:38
  12.8 60.1 %collective-permute-start.1 = (f32[1,127,64]{1,2,0:T(8,128)}, f32[1,127,64]{1,2,0:T(8,128)}, u32[]{:S(2)}, u32[]{:S(2)}) collective-permute-start(f32[1,127,64]{1,2,0:T(8,128)} %bitcast.12), channel_id=1, source_target_pairs={{1,0},{2,1},{3,2},{4,3},{5,4},{6,5},{7,6},{8,7},{9,8},{10,9},{11,1... | collective-permute-start | bytes 97544 | tf_op jit(solution)/shard_map/ppermute | solution.py:39
  31.2 8.0 %copy-start.67 = (f32[5]{0:T(128)S(1)}, f32[5]{0:T(128)}, u32[]{:S(2)}) copy-start(f32[5]{0:T(128)} %constant.232.clone) | copy-start | bytes 64
  31.3 16.7 %copy-start.18 = (s32[6,512]{1,0:T(8,128)S(1)}, s32[6,512]{1,0:T(8,128)}, u32[]{:S(2)}) copy-start(s32[6,512]{1,0:T(8,128)} %param.15) | copy-start | bytes 36868
  52.4 74.0 %copy-start.21 = (s32[1024]{0:T(1024)}, s32[1024]{0:T(1024)S(1)}, u32[]{:S(2)}) copy-start(s32[1024]{0:T(1024)S(1)} %pad_clamp_fusion.7) | copy-start | bytes 12292
  59.2 62.4 %copy-start.26 = (s32[1024]{0:T(1024)}, s32[1024]{0:T(1024)S(1)}, u32[]{:S(2)}) copy-start(s32[1024]{0:T(1024)S(1)} %pad_clamp_fusion.5) | copy-start | bytes 12292
  60.1 5.9 %copy-start.20 = (f32[25,125]{1,0:T(8,128)S(1)}, f32[25,125]{1,0:T(8,128)}, u32[]{:S(2)}) copy-start(f32[25,125]{1,0:T(8,128)} %get-tuple-element.131) | copy-start | bytes 37504
  60.9 33.9 %copy-start.54 = (f32[125]{0:T(128)}, f32[125]{0:T(128)S(1)}, u32[]{:S(2)}) copy-start(f32[125]{0:T(128)S(1)} %mul.1195) | copy-start | bytes 1504
  61.0 33.0 %copy-start.46 = (f32[375]{0:T(512)}, f32[375]{0:T(512)S(1)}, u32[]{:S(2)}) copy-start(f32[375]{0:T(512)S(1)} %mul.1214) | copy-start | bytes 4504
  77.2 9.2 %copy-start.41 = (s32[1024]{0:T(1024)S(1)}, s32[1024]{0:T(1024)}, u32[]{:S(2)}) copy-start(s32[1024]{0:T(1024)} %pad_clamp_fusion) | copy-start | bytes 12292
  77.4 11.5 %copy-start.24 = (s32[1024]{0:T(1024)S(1)}, s32[1024]{0:T(1024)}, u32[]{:S(2)}) copy-start(s32[1024]{0:T(1024)} %pad_clamp_fusion.6) | copy-start | bytes 12292
  78.4 44.4 %collective-permute-start.3 = (f32[1,51,256]{2,1,0:T(8,128)S(1)}, f32[1,51,256]{2,1,0:T(8,128)S(1)}, u32[]{:S(2)}, u32[]{:S(2)}) collective-permute-start(f32[1,51,256]{2,1,0:T(8,128)S(1)} %bitcast.212), channel_id=1, source_target_pairs={{1,0},{2,1},{3,2},{4,3},{5,4},{6,5},{7,6},{8,7},{9,8},{10,9},{11,1... | collective-permute-start | bytes 156680 | tf_op jit(solution)/shard_map/ppermute | solution.py:39
  83.5 6.8 %copy-start.32 = (s32[1024]{0:T(1024)S(1)}, s32[1024]{0:T(1024)}, u32[]{:S(2)}) copy-start(s32[1024]{0:T(1024)} %pad_clamp_fusion.3) | copy-start | bytes 12292
  83.5 39.3 %collective-permute-start.2 = (f32[1,51,256]{2,1,0:T(8,128)}, f32[1,51,256]{2,1,0:T(8,128)S(1)}, u32[]{:S(2)}, u32[]{:S(2)}) collective-permute-start(f32[1,51,256]{2,1,0:T(8,128)} %bitcast.20), channel_id=1, source_target_pairs={{0,1},{1,2},{2,3},{3,4},{4,5},{5,6},{6,7},{7,8},{8,9},{9,10},{10,1... | collective-permute-start | bytes 156680 | tf_op jit(solution)/shard_map/ppermute | solution.py:38
  95.6 9.3 %copy-start.35 = (s32[1024]{0:T(1024)S(1)}, s32[1024]{0:T(1024)}, u32[]{:S(2)}) copy-start(s32[1024]{0:T(1024)} %pad_clamp_fusion.1) | copy-start | bytes 12292
  100.2 9.3 %copy-start.38 = (s32[1024]{0:T(1024)S(1)}, s32[1024]{0:T(1024)}, u32[]{:S(2)}) copy-start(s32[1024]{0:T(1024)} %pad_clamp_fusion.2) | copy-start | bytes 12292
  130.0 7.7 %copy-start.64 = (pred[512]{0:T(512)(128)(4,1)S(1)}, pred[512]{0:T(512)(128)(4,1)}, u32[]{:S(2)}) copy-start(pred[512]{0:T(512)(128)(4,1)} %get-tuple-element.20) | copy-start | bytes 1540
  131.7 6.1 %copy-start.27 = (s32[1024]{0:T(1024)S(1)}, s32[1024]{0:T(1024)}, u32[]{:S(2)}) copy-start(s32[1024]{0:T(1024)} %copy-done.26) | copy-start | bytes 12292
  132.7 5.6 %copy-start.19 = (s32[6,512]{1,0:T(8,128)S(1)}, s32[6,512]{1,0:T(8,128)}, u32[]{:S(2)}) copy-start(s32[6,512]{1,0:T(8,128)} %param.15) | copy-start | bytes 36868
  132.7 5.6 %copy-start.56 = (f32[512]{0:T(512)S(1)}, f32[512]{0:T(512)}, u32[]{:S(2)}) copy-start(f32[512]{0:T(512)} %gather_fusion.37) | copy-start | bytes 6148
  132.8 5.6 %copy-start.57 = (f32[512]{0:T(512)S(1)}, f32[512]{0:T(512)}, u32[]{:S(2)}) copy-start(f32[512]{0:T(512)} %gather_fusion.16) | copy-start | bytes 6148
  132.8 5.6 %copy-start.58 = (f32[512]{0:T(512)S(1)}, f32[512]{0:T(512)}, u32[]{:S(2)}) copy-start(f32[512]{0:T(512)} %gather_fusion.30) | copy-start | bytes 6148
  132.8 5.6 %copy-start.59 = (f32[512]{0:T(512)S(1)}, f32[512]{0:T(512)}, u32[]{:S(2)}) copy-start(f32[512]{0:T(512)} %gather_fusion.23) | copy-start | bytes 6148
  132.8 5.6 %copy-start.60 = (f32[512]{0:T(512)S(1)}, f32[512]{0:T(512)}, u32[]{:S(2)}) copy-start(f32[512]{0:T(512)} %gather_fusion.9) | copy-start | bytes 6148
  132.8 5.6 %copy-start.61 = (f32[512]{0:T(512)S(1)}, f32[512]{0:T(512)}, u32[]{:S(2)}) copy-start(f32[512]{0:T(512)} %gather_fusion.2) | copy-start | bytes 6148
  132.8 6.8 %copy-start.48 = (pred[512]{0:T(512)(128)(4,1)S(1)}, pred[512]{0:T(512)(128)(4,1)}, u32[]{:S(2)}) copy-start(pred[512]{0:T(512)(128)(4,1)} %get-tuple-element.15) | copy-start | bytes 1540
  132.8 6.8 %copy-start.49 = (pred[512]{0:T(512)(128)(4,1)S(1)}, pred[512]{0:T(512)(128)(4,1)}, u32[]{:S(2)}) copy-start(pred[512]{0:T(512)(128)(4,1)} %get-tuple-element.191) | copy-start | bytes 1540
  132.8 6.8 %copy-start.50 = (pred[512]{0:T(512)(128)(4,1)S(1)}, pred[512]{0:T(512)(128)(4,1)}, u32[]{:S(2)}) copy-start(pred[512]{0:T(512)(128)(4,1)} %get-tuple-element.12) | copy-start | bytes 1540
  132.8 6.8 %copy-start.51 = (pred[512]{0:T(512)(128)(4,1)S(1)}, pred[512]{0:T(512)(128)(4,1)}, u32[]{:S(2)}) copy-start(pred[512]{0:T(512)(128)(4,1)} %get-tuple-element.192) | copy-start | bytes 1540
  132.8 6.8 %copy-start.52 = (pred[512]{0:T(512)(128)(4,1)S(1)}, pred[512]{0:T(512)(128)(4,1)}, u32[]{:S(2)}) copy-start(pred[512]{0:T(512)(128)(4,1)} %get-tuple-element.14) | copy-start | bytes 1540
  132.9 6.8 %copy-start.53 = (pred[512]{0:T(512)(128)(4,1)S(1)}, pred[512]{0:T(512)(128)(4,1)}, u32[]{:S(2)}) copy-start(pred[512]{0:T(512)(128)(4,1)} %get-tuple-element.189) | copy-start | bytes 1540
  134.4 6.2 %copy-start.39 = (s32[1024]{0:T(1024)S(1)}, s32[1024]{0:T(1024)}, u32[]{:S(2)}) copy-start(s32[1024]{0:T(1024)} %pad_clamp_fusion.2) | copy-start | bytes 12292
  147.8 8.2 %copy-start.13 = (f32[25,512]{1,0:T(8,128)S(1)}, f32[25,512]{1,0:T(8,128)}, u32[]{:S(2)}) copy-start(f32[25,512]{1,0:T(8,128)} %get-tuple-element.75) | copy-start | bytes 153604
  154.7 6.0 %copy-start.30 = (f32[1,512]{1,0:T(1,128)S(1)}, f32[1,512]{1,0:T(1,128)}, u32[]{:S(2)}) copy-start(f32[1,512]{1,0:T(1,128)} %copy-done.29) | copy-start | bytes 6148
  155.9 6.3 %copy-start.12 = (f32[25,512]{1,0:T(8,128)S(1)}, f32[25,512]{1,0:T(8,128)}, u32[]{:S(2)}) copy-start(f32[25,512]{1,0:T(8,128)} %gather_fusion.29) | copy-start | bytes 153604
  157.2 5.9 %copy-start.6 = (f32[25,512]{1,0:T(8,128)S(1)}, f32[25,512]{1,0:T(8,128)}, u32[]{:S(2)}) copy-start(f32[25,512]{1,0:T(8,128)} %gather_fusion.43) | copy-start | bytes 153604
  158.0 6.1 %copy-start.5 = (f32[25,512]{1,0:T(8,128)S(1)}, f32[25,512]{1,0:T(8,128)}, u32[]{:S(2)}) copy-start(f32[25,512]{1,0:T(8,128)} %gather_fusion.22) | copy-start | bytes 153604
  160.1 4.9 %copy-start.7 = (f32[25,512]{1,0:T(8,128)S(1)}, f32[25,512]{1,0:T(8,128)}, u32[]{:S(2)}) copy-start(f32[25,512]{1,0:T(8,128)} %get-tuple-element.63) | copy-start | bytes 153604
  160.1 4.9 %copy-start.8 = (f32[25,512]{1,0:T(8,128)S(1)}, f32[25,512]{1,0:T(8,128)}, u32[]{:S(2)}) copy-start(f32[25,512]{1,0:T(8,128)} %get-tuple-element.64) | copy-start | bytes 153604
  160.1 4.9 %copy-start.9 = (f32[25,512]{1,0:T(8,128)S(1)}, f32[25,512]{1,0:T(8,128)}, u32[]{:S(2)}) copy-start(f32[25,512]{1,0:T(8,128)} %get-tuple-element.65) | copy-start | bytes 153604
  164.9 63.0 %copy-start.47 = (f32[375]{0:T(512)S(1)}, f32[375]{0:T(512)}, u32[]{:S(2)}) copy-start(f32[375]{0:T(512)} %copy-done.46) | copy-start | bytes 4504
  234.6 11.7 %copy-start.40 = (s32[1024]{0:T(1024)S(1)}, s32[1024]{0:T(1024)}, u32[]{:S(2)}) copy-start(s32[1024]{0:T(1024)} %pad_clamp_fusion.2) | copy-start | bytes 12292
  237.7 27.2 %collective-permute-start.5 = (f32[1,51,256]{2,1,0:T(8,128)}, f32[1,51,256]{2,1,0:T(8,128)}, u32[]{:S(2)}, u32[]{:S(2)}) collective-permute-start(f32[1,51,256]{2,1,0:T(8,128)} %bitcast.74), channel_id=1, source_target_pairs={{1,0},{2,1},{3,2},{4,3},{5,4},{6,5},{7,6},{8,7},{9,8},{10,9},{11,1... | collective-permute-start | bytes 156680 | tf_op jit(solution)/shard_map/ppermute | solution.py:39
  240.6 10.1 %copy-start.17 = (f32[25,512]{1,0:T(8,128)S(1)}, f32[25,512]{1,0:T(8,128)}, u32[]{:S(2)}) copy-start(f32[25,512]{1,0:T(8,128)} %gather_fusion.79) | copy-start | bytes 153604
  241.3 24.2 %collective-permute-start.4 = (f32[1,51,256]{2,1,0:T(8,128)}, f32[1,51,256]{2,1,0:T(8,128)}, u32[]{:S(2)}, u32[]{:S(2)}) collective-permute-start(f32[1,51,256]{2,1,0:T(8,128)} %bitcast.71), channel_id=1, source_target_pairs={{0,1},{1,2},{2,3},{3,4},{4,5},{5,6},{6,7},{7,8},{8,9},{9,10},{10,1... | collective-permute-start | bytes 156680 | tf_op jit(solution)/shard_map/ppermute | solution.py:38
  246.2 6.2 %copy-start.28 = (s32[1024]{0:T(1024)S(1)}, s32[1024]{0:T(1024)}, u32[]{:S(2)}) copy-start(s32[1024]{0:T(1024)} %copy-done.26) | copy-start | bytes 12292
  248.6 5.8 %copy-start.36 = (s32[1024]{0:T(1024)S(1)}, s32[1024]{0:T(1024)}, u32[]{:S(2)}) copy-start(s32[1024]{0:T(1024)} %pad_clamp_fusion.1) | copy-start | bytes 12292
  253.7 7.2 %copy-start.33 = (s32[1024]{0:T(1024)S(1)}, s32[1024]{0:T(1024)}, u32[]{:S(2)}) copy-start(s32[1024]{0:T(1024)} %pad_clamp_fusion.3) | copy-start | bytes 12292
  260.8 8.9 %copy-start.23 = (s32[1024]{0:T(1024)S(1)}, s32[1024]{0:T(1024)}, u32[]{:S(2)}) copy-start(s32[1024]{0:T(1024)} %copy-done.21) | copy-start | bytes 12292
  288.4 8.3 %copy-start.31 = (f32[1,512]{1,0:T(1,128)S(1)}, f32[1,512]{1,0:T(1,128)}, u32[]{:S(2)}) copy-start(f32[1,512]{1,0:T(1,128)} %copy-done.29) | copy-start | bytes 6148
  293.5 4.8 %copy-start.37 = (s32[1024]{0:T(1024)S(1)}, s32[1024]{0:T(1024)}, u32[]{:S(2)}) copy-start(s32[1024]{0:T(1024)} %pad_clamp_fusion.1) | copy-start | bytes 12292
  295.2 6.5 %copy-start.15 = (f32[25,512]{1,0:T(8,128)S(1)}, f32[25,512]{1,0:T(8,128)}, u32[]{:S(2)}) copy-start(f32[25,512]{1,0:T(8,128)} %gather_fusion.76) | copy-start | bytes 153604
  295.2 6.5 %copy-start.63 = (pred[512]{0:T(512)(128)(4,1)S(1)}, pred[512]{0:T(512)(128)(4,1)}, u32[]{:S(2)}) copy-start(pred[512]{0:T(512)(128)(4,1)} %get-tuple-element.18) | copy-start | bytes 1540
  298.3 7.4 %copy-start.34 = (s32[1024]{0:T(1024)S(1)}, s32[1024]{0:T(1024)}, u32[]{:S(2)}) copy-start(s32[1024]{0:T(1024)} %pad_clamp_fusion.3) | copy-start | bytes 12292
  303.5 9.0 %copy-start = (f32[25,512]{1,0:T(8,128)S(1)}, f32[25,512]{1,0:T(8,128)}, u32[]{:S(2)}) copy-start(f32[25,512]{1,0:T(8,128)} %gather_fusion.68) | copy-start | bytes 153604
  307.3 8.2 %copy-start.45 = (f32[1,512]{1,0:T(1,128)S(1)}, f32[1,512]{1,0:T(1,128)}, u32[]{:S(2)}) copy-start(f32[1,512]{1,0:T(1,128)} %get-tuple-element.113) | copy-start | bytes 6148
  309.0 7.5 %copy-start.44 = (f32[1,512]{1,0:T(1,128)S(1)}, f32[1,512]{1,0:T(1,128)}, u32[]{:S(2)}) copy-start(f32[1,512]{1,0:T(1,128)} %get-tuple-element.114) | copy-start | bytes 6148
  311.1 6.2 %copy-start.2 = (f32[25,512]{1,0:T(8,128)S(1)}, f32[25,512]{1,0:T(8,128)}, u32[]{:S(2)}) copy-start(f32[25,512]{1,0:T(8,128)} %get-tuple-element.57) | copy-start | bytes 153604
  311.1 6.2 %copy-start.3 = (f32[25,512]{1,0:T(8,128)S(1)}, f32[25,512]{1,0:T(8,128)}, u32[]{:S(2)}) copy-start(f32[25,512]{1,0:T(8,128)} %get-tuple-element.58) | copy-start | bytes 153604
  311.1 6.2 %copy-start.4 = (f32[25,512]{1,0:T(8,128)S(1)}, f32[25,512]{1,0:T(8,128)}, u32[]{:S(2)}) copy-start(f32[25,512]{1,0:T(8,128)} %get-tuple-element.59) | copy-start | bytes 153604
  311.7 4.8 %copy-start.10 = (f32[25,512]{1,0:T(8,128)S(1)}, f32[25,512]{1,0:T(8,128)}, u32[]{:S(2)}) copy-start(f32[25,512]{1,0:T(8,128)} %gather_fusion.77) | copy-start | bytes 153604
  311.7 4.8 %copy-start.11 = (f32[25,512]{1,0:T(8,128)S(1)}, f32[25,512]{1,0:T(8,128)}, u32[]{:S(2)}) copy-start(f32[25,512]{1,0:T(8,128)} %gather_fusion.59) | copy-start | bytes 153604
  (11 other events, 34.7 us)
where the time goes:
time: 385 us; the launch traced here: 381 us
  local copies, waits for them, and re-layouts  182 us (47%)
  blocking collectives  109 us (28%)
  other arithmetic  42.4 us (11%)
  starting transfers between devices  32.7 us (8%)
  between operations  8.27 us (2%)
  matrix products  6.82 us (2%)
    psum x8, blocking collectives, by_axis(): return functools.reduce(lax.psum, axes, shard)  109 us
    gather x8, local copies, waits for them, and re-layouts, operate(): near_conduct = other_conduct[safe_idx]  32.3 us
    gather x24, local copies, waits for them, and re-layouts, operate(): near_value = other_value[:, safe_idx]  23.4 us
    gather x24, local copies, waits for them, and re-layouts, operate(): near_flux = other_flux[:, safe_idx]  23.4 us
    ppermute x3, starting transfers between devices, with_halo(): lax.ppermute(initial, axis, [(b, a) for a, b in up])  22.6 us
    gather x12, local copies, waits for them, and re-layouts, operate(): near_flux = jnp.where(second_bit, near_flux[flip_second], near_flux)  14.5 us
    gather x12, local copies, waits for them, and re-layouts, operate(): near_flux = jnp.where(first_bit, near_flux[flip_first], near_flux)  10.3 us
    ppermute x3, starting transfers between devices, with_halo(): lax.ppermute(last, axis, up)  10.1 us
  transfers between devices with their start and end apart: 6, of which 0 were waited for; matrix products, arithmetic and copies ran while one was open for 27% of the time, Pallas kernels for 0%

commit v1 on v0

v1 whole, which is shorter than its diff:
```python
import functools

import jax
import jax.numpy as jnp
import ml_dtypes
import numpy as np
from jax import lax
from jax.experimental import pallas as pl
from jax.experimental.pallas import tpu as pltpu
from jax.sharding import PartitionSpec as P

NODES = 5
BLOCK = 125
CELLS = 512
GHOST = 256
MOVE = 64
PENALTY = 80.0
FACE = 64
HALF = 32
ROWS = 128
X_SIZE = 8
MESH = pl.DeviceIdType.MESH
F32 = jnp.float32
BF16 = jnp.bfloat16
CURVE_GROUP = ("curve", "group")
GAUSS_POINTS = (-0.906179845938664, -0.5384693101056831, 0.0, 0.5384693101056831, 0.906179845938664)
GAUSS_WEIGHTS = (
    0.2369268850561891,
    0.4786286704993665,
    0.5688888888888889,
    0.4786286704993665,
    0.2369268850561891,
)


def lagrange_value(points, position, location):
    product_value = 1.0
    for other in range(len(points)):
        if other != position:
            product_value *= (location - points[other]) / (points[position] - points[other])
    return product_value


def lagrange_slope(points, position, location):
    slope_sum = 0.0
    for skipped in range(len(points)):
        if skipped == position:
            continue
        addend = 1.0 / (points[position] - points[skipped])
        for other in range(len(points)):
            if other != position and other != skipped:
                addend *= (location - points[other]) / (points[position] - points[other])
        slope_sum += addend
    return slope_sum


def along_axis(matrix, axis_id):
    eye = np.eye(NODES)
    parts = [eye, eye, eye]
    parts[axis_id] = matrix
    return np.kron(parts[0], np.kron(parts[1], parts[2]))


def tables():
    points = [0.5 * (value + 1.0) for value in GAUSS_POINTS]
    weights = np.array([0.5 * value for value in GAUSS_WEIGHTS])
    slopes = np.array([[lagrange_slope(points, p, points[q]) for p in range(NODES)] for q in range(NODES)])
    ends = [
        (
            np.array([lagrange_value(points, p, 0.0) for p in range(NODES)]),
            np.array([-lagrange_slope(points, p, 0.0) for p in range(NODES)]),
        ),
        (
            np.array([lagrange_value(points, p, 1.0) for p in range(NODES)]),
            np.array([lagrange_slope(points, p, 1.0) for p in range(NODES)]),
        ),
    ]
    cell_weight = np.kron(weights, np.kron(weights, weights))
    volume = sum(
        along_axis(slopes, a).T @ (cell_weight[:, None] * along_axis(slopes, a)) for a in range(3)
    )
    root = np.sqrt(0.5)
    modes = np.array(
        [
            [root, 0, 0, 0, root],
            [0, root, 0, root, 0],
            [0, 0, 1, 0, 0],
            [root, 0, 0, 0, -root],
            [0, root, 0, -root, 0],
        ]
    )
    modes = np.kron(modes, modes)
    mode_weight = np.array([weights[0], weights[1], weights[2], weights[0], weights[1]])
    mode_weight = np.kron(mode_weight, mode_weight)
    forward = np.zeros((6 * FACE + ROWS, ROWS))
    backward = np.zeros((ROWS, 6 * FACE))
    for face in range(6):
        trace, normal = ends[face % 2]
        trace = modes @ along_axis(trace[None, :], face // 2)
        normal = modes @ along_axis(normal[None, :], face // 2)
        row = face * FACE
        forward[row : row + 25, :BLOCK] = trace
        forward[row + 25, BLOCK] = 1.0
        forward[row + HALF : row + HALF + 25, :BLOCK] = normal
        backward[:BLOCK, row : row + 25] = trace.T * mode_weight
        backward[:BLOCK, row + HALF : row + HALF + 25] = -0.5 * normal.T * mode_weight
    forward[6 * FACE : 6 * FACE + BLOCK, :BLOCK] = volume
    weight_rows = np.zeros((ROWS, 1))
    weight_rows[:BLOCK, 0] = cell_weight

    def halves(table):
        high = table.astype(ml_dtypes.bfloat16)
        return high, (table - high.astype(np.float64)).astype(ml_dtypes.bfloat16)

    fwd_high, fwd_low = halves(forward)
    back_high, back_low = halves(backward)
    return (
        np.concatenate([fwd_high, fwd_high], 1),
        fwd_low,
        back_high,
        back_low,
        np.broadcast_to(weight_rows, (ROWS, 128)).astype(np.float32),
    )


def dot_nn(left, right):
    return jnp.dot(left, right, preferred_element_type=F32)


def dot_nt(left, right):
    return lax.dot_general(left, right, (((1,), (1,)), ((), ())), preferred_element_type=F32)


def split2(value):
    high = value.astype(BF16)
    return high, (value - high.astype(F32)).astype(BF16)


def split3(value):
    high = value.astype(BF16)
    rest = value - high.astype(F32)
    mid = rest.astype(BF16)
    return high, mid, (rest - mid.astype(F32)).astype(BF16)


def onehot(index_row, rows, start=0):
    ids = lax.broadcasted_iota(jnp.int32, (rows, index_row.shape[1]), 0) + start
    return jnp.where(ids == index_row, 1.0, 0.0).astype(BF16)


def kernel(
    n_curve, n_group, x_size,
    rs_ref, cond_ref, dest_ref, nb_ref, ori_ref, sl_ref, fa_ref, fb_ref, bh_ref, bl_ref, w_ref,
    b_out, y_out, z_out, coef_out,
    x_ref, x3_ref, q_ref, g_ref, gg_ref, s_ref, sign_ref, f_ref, fs_ref, ch_ref, cl_ref,
    mig_send, mig_recv, halo_send, halo_recv, row_send, curve_recv, x_recv, z_recv,
    mig_ssem, mig_rsem, halo_ssem, halo_rsem, curve_ssem, curve_rsem, x_ssem, x_rsem, z_ssem, z_rsem,
):
    curve = lax.axis_index("curve")
    group = lax.axis_index("group")
    me = curve * n_group + group
    total = n_curve * n_group
    left_rank = lax.rem(me + total - 1, total)
    right_rank = lax.rem(me + 1, total)

    def device(rank):
        return (rank // n_group, lax.rem(rank, n_group))

    left, right = device(left_rank), device(right_rank)
    z_size = n_group // x_size
    x_pos = lax.rem(group, x_size)
    z_pos = group // x_size
    curve_peers = [(lax.rem(curve + d, n_curve), group) for d in range(1, n_curve)]
    x_peers = [(curve, z_pos * x_size + lax.rem(x_pos + d, x_size)) for d in range(1, x_size)]
    z_peers = [(curve, lax.rem(z_pos + d, z_size) * x_size + x_pos) for d in range(1, z_size)]
    everyone = [left, right] + curve_peers + x_peers + z_peers

    barrier = pltpu.get_barrier_semaphore()
    for peer in everyone:
        pl.semaphore_signal(barrier, inc=1, device_id=peer, device_id_type=MESH)

    destination = dest_ref[...]
    target = lax.shift_right_arithmetic(destination, 9) - me
    slot = jnp.bitwise_and(destination, CELLS - 1)
    x_ref[0:BLOCK, :] = rs_ref[...]
    x_ref[BLOCK : BLOCK + 1, :] = cond_ref[...]
    x_ref[BLOCK + 1 : BLOCK + 2, :] = (slot + 1).astype(F32)
    x_ref[BLOCK + 2 : ROWS, :] = jnp.zeros((ROWS - BLOCK - 2, CELLS), F32)
    high, mid, low = split3(x_ref[...])
    x3_ref[0:ROWS, :] = high
    x3_ref[ROWS : 2 * ROWS, :] = mid
    x3_ref[2 * ROWS : 3 * ROWS, :] = low
    row8 = lax.broadcasted_iota(jnp.int32, (8, CELLS), 0)
    leaving = jnp.where(((row8 == 0) & (target == -1)) | ((row8 == 1) & (target == 1)), 1.0, 0.0)
    for start in range(0, CELLS, 64):
        ids = lax.broadcasted_iota(jnp.int32, (64, CELLS), 0) + start
        lanes = lax.broadcasted_iota(jnp.int32, (64, CELLS), 1)
        q_ref[start : start + 64, :] = jnp.where(ids <= lanes, 1.0, 0.0).astype(BF16)
    counts = dot_nn(leaving.astype(BF16), q_ref[...]).astype(jnp.int32)
    place = jnp.where(target == -1, counts[0:1] - 1, jnp.where(target == 1, counts[1:2] + (MOVE - 1), -1))
    packed = dot_nt(onehot(place, 2 * MOVE), x3_ref[...])
    mig_send[...] = packed[:, 0:ROWS] + packed[:, ROWS : 2 * ROWS] + packed[:, 2 * ROWS :]

    pl.semaphore_wait(barrier, len(everyone))

    def copy(source, sink, ssem, rsem, peer):
        return pltpu.make_async_remote_copy(
            src_ref=source, dst_ref=sink, send_sem=ssem, recv_sem=rsem, device_id=peer, device_id_type=MESH
        )

    to_left = copy(
        mig_send.at[pl.ds(0, MOVE)], mig_recv.at[pl.ds(MOVE, MOVE)], mig_ssem.at[0], mig_rsem.at[0], left
    )
    to_right = copy(
        mig_send.at[pl.ds(MOVE, MOVE)], mig_recv.at[pl.ds(0, MOVE)], mig_ssem.at[1], mig_rsem.at[1], right
    )
    to_left.start()
    to_right.start()

    staying = jnp.where(target == 0, slot, -1)
    for start in range(0, CELLS, 64):
        q_ref[start : start + 64, :] = onehot(staying, 64, start)
    stay = dot_nt(x3_ref[...], q_ref[...])
    f_ref[0:ROWS, :] = stay[0:ROWS] + stay[ROWS : 2 * ROWS] + stay[2 * ROWS :]

    for side in range(2):
        for start in range(0, CELLS, 128):
            s_ref[side, start : start + 128, :] = onehot(sl_ref[side : side + 1, :], 128, start)
    mode = lax.broadcasted_iota(jnp.int32, (HALF, CELLS), 0)
    odd_first = jnp.where((mode >= 15) & (mode < 25), 2.0, 0.0)
    second = functools.reduce(jnp.logical_or, [mode == 5 * i + j for i in range(5) for j in (3, 4)])
    odd_second = jnp.where(second, 2.0, 0.0)
    outside = []
    for face in range(6):
        partner = nb_ref[face : face + 1, :]
        outside.append(jnp.where(partner < 0, 2.0, 1.0))
        for start in range(0, CELLS, 64):
            g_ref[face, start : start + 64, :] = onehot(partner, 64, start)
        if face < 2:
            for start in range(0, GHOST, 64):
                gg_ref[face, start : start + 64, :] = onehot(partner, 64, CELLS + face * GHOST + start)
        code = ori_ref[face : face + 1, :]
        first_bit = jnp.bitwise_and(code, 1).astype(F32)
        second_bit = lax.shift_right_arithmetic(code, 1).astype(F32)
        sign_ref[face] = (1.0 - odd_first * first_bit) * (1.0 - odd_second * second_bit)

    to_left.wait_recv()
    to_right.wait_recv()
    arrived = mig_recv[...].T
    place_in = arrived[BLOCK + 1 : BLOCK + 2, :].astype(jnp.int32) - 1
    for start in range(0, CELLS, 128):
        q_ref[start : start + 128, 0 : 2 * MOVE] = onehot(place_in, 128, start)
    parts = jnp.concatenate(split3(arrived), 0)
    moved = dot_nt(parts, q_ref[:, 0 : 2 * MOVE])
    field = f_ref[0:ROWS, :] + (moved[0:ROWS] + moved[ROWS : 2 * ROWS] + moved[2 * ROWS :])
    conduct = field[BLOCK : BLOCK + 1, :]
    row_ids = lax.broadcasted_iota(jnp.int32, (ROWS, CELLS), 0)
    source = jnp.where(row_ids < BLOCK, field, 0.0)
    b_out[...] = source

    def operate(value, step):
        high, low = split2(jnp.where(row_ids == BLOCK, conduct, value))
        both = jnp.concatenate([high, low], 0)

        def forward(start, stop):
            rows = pl.ds(start, stop - start)
            f_ref[rows, :] = dot_nn(fa_ref[rows, :], both) + dot_nn(fb_ref[rows, :], high)

        def stack(face):
            high, low = split2(f_ref[face * FACE : (face + 1) * FACE, :])
            fs_ref[face, 0:FACE, :] = high
            fs_ref[face, FACE : 2 * FACE, :] = low

        def pair(product):
            return product[0:FACE] + product[FACE : 2 * FACE]

        copies = []
        forward(0, 2 * FACE)
        for side, peer in ((0, left), (1, right)):
            stack(side)
            halo_send[step, side] = pair(dot_nn(fs_ref[side], s_ref[side]))
            copies.append(
                copy(
                    halo_send.at[step, side], halo_recv.at[step, 1 - side],
                    halo_ssem.at[step, side], halo_rsem.at[step, side], peer,
                )
            )
            copies[-1].start()
        forward(2 * FACE, 6 * FACE + ROWS)
        for face in range(2, 6):
            stack(face)

        def coefficients(face, near):
            row = face * FACE
            trace = f_ref[row : row + HALF, :]
            normal = f_ref[row + HALF : row + FACE, :]
            near_conduct = near[25:26, :]
            sign = sign_ref[face]
            near_value = sign * near[0:HALF]
            near_normal = sign * near[HALF:FACE]
            penalty = PENALTY * jnp.maximum(conduct, near_conduct)
            jump = outside[face] * trace - near_value
            first = (
                penalty * jump
                - (0.5 * outside[face] * conduct) * normal
                + (0.5 * near_conduct) * near_normal
            )
            for offset, part in ((0, first), (HALF, conduct * jump)):
                high, low = split2(part)
                ch_ref[row + offset : row + offset + HALF, :] = high
                cl_ref[row + offset : row + offset + HALF, :] = low

        def backward(start, stop):
            columns = slice(start * FACE, stop * FACE)
            back_high = bh_ref[:, columns]
            return (
                dot_nn(back_high, ch_ref[columns, :])
                + dot_nn(back_high, cl_ref[columns, :])
                + dot_nn(bl_ref[:, columns], ch_ref[columns, :])
            )

        for face in range(2, 6):
            coefficients(face, pair(dot_nn(fs_ref[face ^ 1], g_ref[face])))
        local = [pair(dot_nn(fs_ref[face ^ 1], g_ref[face])) for face in range(2)]
        result = w_ref[:, 0:1] * value + conduct * f_ref[6 * FACE :, :] + backward(2, 6)
        for face in range(2):
            copies[1 - face].wait_recv()
            high, low = split2(halo_recv[step, face])
            ghost = pair(dot_nn(jnp.concatenate([high, low], 0), gg_ref[face]))
            coefficients(face, local[face] + ghost)
        return result + backward(0, 2), copies

    image, copies_one = operate(source, 0)
    y_out[...] = image
    second_image, copies_two = operate(image, 1)
    z_out[...] = second_image

    source = b_out[...]
    image = y_out[...]
    lane = lax.broadcasted_iota(jnp.int32, (1, 128), 1)
    row = jnp.zeros((1, 128), F32)
    for index, terms in enumerate(
        (source * source, source * image, image * image, source * second_image, image * second_image)
    ):
        row = row + jnp.where(lane == index, jnp.sum(terms, axis=(0, 1), keepdims=True), 0.0)

    sent = []
    for phase, (peers, landing, ssem, rsem) in enumerate(
        (
            (curve_peers, curve_recv, curve_ssem, curve_rsem),
            (x_peers, x_recv, x_ssem, x_rsem),
            (z_peers, z_recv, z_ssem, z_rsem),
        )
    ):
        row_send[phase] = row
        out = [
            copy(row_send.at[phase], landing.at[i], ssem.at[i], rsem.at[i], peer)
            for i, peer in enumerate(peers)
        ]
        for one in out:
            one.start()
        for i, one in enumerate(out):
            one.wait_recv()
            row = row + landing[i]
        sent += out

    bb, by, yy, bz, yz = (
        jnp.sum(jnp.where(lane == index, row, 0.0), axis=1, keepdims=True) for index in range(5)
    )
    alpha = bb / by
    norm_next = bb - alpha * (2.0 * by - alpha * yy)
    beta = norm_next / bb
    grow = 1.0 + beta
    curvature = grow * (grow * by - alpha * (bz + yy)) + alpha * (alpha * yz)
    alpha_next = norm_next / curvature
    coef_out[0:1, :] = jnp.broadcast_to(alpha + alpha_next * grow, (1, 128))
    coef_out[1:2, :] = jnp.broadcast_to(alpha * alpha_next, (1, 128))
    for one in [to_left, to_right] + copies_one + copies_two + sent:
        one.wait_send()


def solution(mesh):
    n_curve, n_group = mesh.shape["curve"], mesh.shape["group"]
    x_size = min(X_SIZE, n_group)
    z_size = n_group // x_size
    constants = tables()
    field = jax.ShapeDtypeStruct((ROWS, CELLS), F32)
    call = pl.pallas_call(
        functools.partial(kernel, n_curve, n_group, x_size),
        out_shape=(field, field, field, jax.ShapeDtypeStruct((2, 128), F32)),
        in_specs=[pl.BlockSpec(memory_space=pltpu.VMEM)] * 11,
        out_specs=[pl.BlockSpec(memory_space=pltpu.VMEM)] * 4,
        scratch_shapes=[
            pltpu.VMEM((ROWS, CELLS), F32),
            pltpu.VMEM((3 * ROWS, CELLS), BF16),
            pltpu.VMEM((CELLS, CELLS), BF16),
            pltpu.VMEM((6, CELLS, CELLS), BF16),
            pltpu.VMEM((2, GHOST, CELLS), BF16),
            pltpu.VMEM((2, CELLS, GHOST), BF16),
            pltpu.VMEM((6, HALF, CELLS), F32),
            pltpu.VMEM((6 * FACE + ROWS, CELLS), F32),
            pltpu.VMEM((6, 2 * FACE, CELLS), BF16),
            pltpu.VMEM((6 * FACE, CELLS), BF16),
            pltpu.VMEM((6 * FACE, CELLS), BF16),
            pltpu.VMEM((2 * MOVE, ROWS), F32),
            pltpu.VMEM((2 * MOVE, ROWS), F32),
            pltpu.VMEM((2, 2, FACE, GHOST), F32),
            pltpu.VMEM((2, 2, FACE, GHOST), F32),
            pltpu.VMEM((3, 1, 128), F32),
            pltpu.VMEM((n_curve - 1, 1, 128), F32),
            pltpu.VMEM((x_size - 1, 1, 128), F32),
            pltpu.VMEM((z_size - 1, 1, 128), F32),
            pltpu.SemaphoreType.DMA((2,)),
            pltpu.SemaphoreType.DMA((2,)),
            pltpu.SemaphoreType.DMA((2, 2)),
            pltpu.SemaphoreType.DMA((2, 2)),
            pltpu.SemaphoreType.DMA((n_curve - 1,)),
            pltpu.SemaphoreType.DMA((n_curve - 1,)),
            pltpu.SemaphoreType.DMA((x_size - 1,)),
            pltpu.SemaphoreType.DMA((x_size - 1,)),
            pltpu.SemaphoreType.DMA((z_size - 1,)),
            pltpu.SemaphoreType.DMA((z_size - 1,)),
        ],
        compiler_params=pltpu.CompilerParams(collective_id=0, has_side_effects=True),
    )

    def body(right_side, conductivity, destination, neighbour, orientation, send_list):
        b, y, z, coef = call(
            right_side, conductivity[None], destination[None], neighbour, orientation, send_list,
            *[jnp.asarray(table) for table in constants],
        )
        b, y, z = b[:BLOCK], y[:BLOCK], z[:BLOCK]
        first, second = coef[0, 0], coef[1, 0]
        return first * b - second * y, b - first * y + second * z

    in_specs = (
        P(None, CURVE_GROUP),
        P(CURVE_GROUP),
        P(CURVE_GROUP),
        P(None, CURVE_GROUP),
        P(None, CURVE_GROUP),
        P(None, CURVE_GROUP),
    )
    out_specs = (P(None, CURVE_GROUP), P(None, CURVE_GROUP))
    return jax.shard_map(body, mesh=mesh, in_specs=in_specs, out_specs=out_specs, check_vma=False)
```

time: 385 us -> 58.6 us (0.15)
  the two profiles are of different devices: /device:TPU:16 before, /device:TPU:2 now
where the time goes in v1:
time: 58.6 us; the launch traced here: 58.4 us
  Pallas kernels  53.3 us (91%)
  other arithmetic  3.23 us (6%)
  local copies, waits for them, and re-layouts  1.2 us (2%)
  between operations  0.65 us (1%)
    pallas_call x1, Pallas kernels, body(): call(right_side, conductivity[None], destination[None], neighbour, orient...  53.3 us
    add x1, other arithmetic, body(): return (first * b - second * y, b - first * y + second * z)  3.23 us

profile of v1, /device:TPU:2, one launch (start us, length us, event | category | flops | bytes accessed | tf_op | source)
XLA Modules:
  0.0 58.4 jit_solution(3644321809540636162)
XLA Ops:
  0.6 53.3 %shard_map.122 = (f32[128,512]{1,0:T(8,128)}, f32[128,512]{1,0:T(8,128)}, f32[128,512]{1,0:T(8,128)}, f32[2,128]{1,0:T(2,128)}) custom-call(f32[125,512]{1,0:T(8,128)} %rs_ref.1, f32[1,512]{1,0:T(1,128)} %bitcast.4, s32[1,512]{1,0:T(1,128)} %bitcast.5, s32[6,512]{1,0:T(8,128)} %nb_ref.1, s32[6,512]{1,0:T(8,128)} %ori_ref.1, s32[2,256]{1,0:T(2,128)} %sl_ref.1, ...), custom_call_target="tpu_custom_call" | custom-call | tf_op jit(solution)/shard_map/pallas_call | solution.py:428
  53.9 0.0 copy-start
  53.9 0.6 %copy-done = f32[2,128]{1,0:T(2,128)S(1)} copy-done((f32[2,128]{1,0:T(2,128)S(1)}, f32[2,128]{1,0:T(2,128)}, u32[]{:S(2)}) %copy-start) | copy-done | bytes 1048
  54.6 0.6 fusion
  55.1 3.2 %multiply_add_fusion = (f32[125,512]{1,0:T(8,128)}, f32[125,512]{1,0:T(8,128)}) fusion(f32[128,512]{1,0:T(8,128)} %get-tuple-element.9, f32[128,512]{1,0:T(8,128)} %get-tuple-element.8, f32[128,512]{1,0:T(8,128)} %get-tuple-element.7, f32[]{:T(128)} %bitcast.3, f32[]{:T(128)} %bitcast.2), kind=kLoop, calls=%fused_computation | loop fusion | flops 448000 | bytes 1280008 | tf_op jit(solution)/shard_map/add | solution.py:434
Async XLA Ops:
  53.9 0.6 %copy-start = (f32[2,128]{1,0:T(2,128)S(1)}, f32[2,128]{1,0:T(2,128)}, u32[]{:S(2)}) copy-start(f32[2,128]{1,0:T(2,128)} %get-tuple-element.6) | copy-start | bytes 3076

commit v2 on v1

--- a/solution.py
+++ b/solution.py
@@ -150,9 +150,10 @@
 
 def kernel(
     n_curve, n_group, x_size,
-    rs_ref, cond_ref, dest_ref, nb_ref, ori_ref, sl_ref, fa_ref, fb_ref, bh_ref, bl_ref, w_ref,
-    b_out, y_out, z_out, coef_out,
-    x_ref, x3_ref, q_ref, g_ref, gg_ref, s_ref, sign_ref, f_ref, fs_ref, ch_ref, cl_ref,
+    rs_hbm, cond_hbm, dest_hbm, nb_hbm, ori_hbm, sl_hbm, fa_hbm, fb_hbm, bh_hbm, bl_hbm, w_hbm,
+    solution_out, residual_out,
+    rs_ref, cond_ref, dest_ref, nb_ref, ori_ref, sl_ref, fa_ref, fb_ref, bh_ref, bl_ref, w_ref, load_sem,
+    b_ref, y_ref, tail_ref, x3_ref, q_ref, g_ref, gg_ref, s_ref, sign_ref, f_ref, fs_ref, ch_ref, cl_ref,
     mig_send, mig_recv, halo_send, halo_recv, row_send, curve_recv, x_recv, z_recv,
     mig_ssem, mig_rsem, halo_ssem, halo_rsem, curve_ssem, curve_rsem, x_ssem, x_rsem, z_ssem, z_rsem,
 ):
@@ -160,62 +161,107 @@
     group = lax.axis_index("group")
     me = curve * n_group + group
     total = n_curve * n_group
-    left_rank = lax.rem(me + total - 1, total)
-    right_rank = lax.rem(me + 1, total)
+    has_left, has_right = me > 0, me < total - 1
 
     def device(rank):
         return (rank // n_group, lax.rem(rank, n_group))
 
-    left, right = device(left_rank), device(right_rank)
+    left, right = device(lax.rem(me + total - 1, total)), device(lax.rem(me + 1, total))
     z_size = n_group // x_size
     x_pos = lax.rem(group, x_size)
     z_pos = group // x_size
     curve_peers = [(lax.rem(curve + d, n_curve), group) for d in range(1, n_curve)]
     x_peers = [(curve, z_pos * x_size + lax.rem(x_pos + d, x_size)) for d in range(1, x_size)]
     z_peers = [(curve, lax.rem(z_pos + d, z_size) * x_size + x_pos) for d in range(1, z_size)]
-    everyone = [left, right] + curve_peers + x_peers + z_peers
+    everyone = curve_peers + x_peers + z_peers
 
     barrier = pltpu.get_barrier_semaphore()
     for peer in everyone:
         pl.semaphore_signal(barrier, inc=1, device_id=peer, device_id_type=MESH)
 
-    destination = dest_ref[...]
-    target = lax.shift_right_arithmetic(destination, 9) - me
-    slot = jnp.bitwise_and(destination, CELLS - 1)
-    x_ref[0:BLOCK, :] = rs_ref[...]
-    x_ref[BLOCK : BLOCK + 1, :] = cond_ref[...]
-    x_ref[BLOCK + 1 : BLOCK + 2, :] = (slot + 1).astype(F32)
-    x_ref[BLOCK + 2 : ROWS, :] = jnp.zeros((ROWS - BLOCK - 2, CELLS), F32)
-    high, mid, low = split3(x_ref[...])
-    x3_ref[0:ROWS, :] = high
-    x3_ref[ROWS : 2 * ROWS, :] = mid
-    x3_ref[2 * ROWS : 3 * ROWS, :] = low
-    row8 = lax.broadcasted_iota(jnp.int32, (8, CELLS), 0)
-    leaving = jnp.where(((row8 == 0) & (target == -1)) | ((row8 == 1) & (target == 1)), 1.0, 0.0)
+    @pl.when(has_left)
+    def _():
+        pl.semaphore_signal(barrier, inc=1, device_id=left, device_id_type=MESH)
+
+    @pl.when(has_right)
+    def _():
+        pl.semaphore_signal(barrier, inc=1, device_id=right, device_id_type=MESH)
+
+    loads = {}
+    for i, (name, source, sink) in enumerate(
+        (
+            ("dest", dest_hbm, dest_ref),
+            ("rs", rs_hbm, rs_ref),
+            ("cond", cond_hbm, cond_ref),
+            ("nb", nb_hbm, nb_ref),
+            ("sl", sl_hbm, sl_ref),
+            ("ori", ori_hbm, ori_ref),
+            ("fa", fa_hbm, fa_ref),
+            ("fb", fb_hbm, fb_ref),
+            ("bh", bh_hbm, bh_ref),
+            ("bl", bl_hbm, bl_ref),
+            ("w", w_hbm, w_ref),
+        )
+    ):
+        loads[name] = pltpu.make_async_copy(source, sink, load_sem.at[i])
+        loads[name].start()
     for start in range(0, CELLS, 64):
         ids = lax.broadcasted_iota(jnp.int32, (64, CELLS), 0) + start
         lanes = lax.broadcasted_iota(jnp.int32, (64, CELLS), 1)
         q_ref[start : start + 64, :] = jnp.where(ids <= lanes, 1.0, 0.0).astype(BF16)
+
+    @pl.when(jnp.logical_not(has_left))
+    def _():
+        mig_recv[0:MOVE, :] = jnp.zeros((MOVE, ROWS), F32)
+        halo_recv[:, 0] = jnp.zeros((2, FACE, GHOST), F32)
+
+    @pl.when(jnp.logical_not(has_right))
+    def _():
+        mig_recv[MOVE:, :] = jnp.zeros((MOVE, ROWS), F32)
+        halo_recv[:, 1] = jnp.zeros((2, FACE, GHOST), F32)
+
+    loads["dest"].wait()
+
+    destination = dest_ref[...]
+    target = lax.shift_right_arithmetic(destination, 9) - me
+    slot = jnp.bitwise_and(destination, CELLS - 1)
+    row8 = lax.broadcasted_iota(jnp.int32, (8, CELLS), 0)
+    leaving = jnp.where(((row8 == 0) & (target == -1)) | ((row8 == 1) & (target == 1)), 1.0, 0.0)
     counts = dot_nn(leaving.astype(BF16), q_ref[...]).astype(jnp.int32)
     place = jnp.where(target == -1, counts[0:1] - 1, jnp.where(target == 1, counts[1:2] + (MOVE - 1), -1))
+    loads["rs"].wait()
+    loads["cond"].wait()
+    tail_ref[0:13, :] = rs_ref[112:BLOCK, :]
+    tail_ref[13:14, :] = cond_ref[...]
+    tail_ref[14:15, :] = (slot + 1).astype(F32)
+    tail_ref[15:16, :] = jnp.zeros((1, CELLS), F32)
+    for start, stop, value in ((0, 112, rs_ref[0:112, :]), (112, ROWS, tail_ref[...])):
+        for i, part in enumerate(split3(value)):
+            x3_ref[i * ROWS + start : i * ROWS + stop, :] = part
     packed = dot_nt(onehot(place, 2 * MOVE), x3_ref[...])
     mig_send[...] = packed[:, 0:ROWS] + packed[:, ROWS : 2 * ROWS] + packed[:, 2 * ROWS :]
 
-    pl.semaphore_wait(barrier, len(everyone))
+    pl.semaphore_wait(barrier, len(everyone) + has_left.astype(jnp.int32) + has_right.astype(jnp.int32))
 
     def copy(source, sink, ssem, rsem, peer):
         return pltpu.make_async_remote_copy(
             src_ref=source, dst_ref=sink, send_sem=ssem, recv_sem=rsem, device_id=peer, device_id_type=MESH
         )
 
+    def start_both(to_left, to_right):
+        pl.when(has_left)(to_left.start)
+        pl.when(has_right)(to_right.start)
+
     to_left = copy(
         mig_send.at[pl.ds(0, MOVE)], mig_recv.at[pl.ds(MOVE, MOVE)], mig_ssem.at[0], mig_rsem.at[0], left
     )
     to_right = copy(
         mig_send.at[pl.ds(MOVE, MOVE)], mig_recv.at[pl.ds(0, MOVE)], mig_ssem.at[1], mig_rsem.at[1], right
     )
-    to_left.start()
-    to_right.start()
+    start_both(to_left, to_right)
+    loads["nb"].wait()
+    loads["sl"].wait()
+    loads["ori"].wait()
 
     staying = jnp.where(target == 0, slot, -1)
     for start in range(0, CELLS, 64):
@@ -244,8 +290,10 @@
         second_bit = lax.shift_right_arithmetic(code, 1).astype(F32)
         sign_ref[face] = (1.0 - odd_first * first_bit) * (1.0 - odd_second * second_bit)
 
-    to_left.wait_recv()
-    to_right.wait_recv()
+    for name in ("fa", "fb", "bh", "bl", "w"):
+        loads[name].wait()
+    pl.when(has_left)(to_right.wait_recv)
+    pl.when(has_right)(to_left.wait_recv)
     arrived = mig_recv[...].T
     place_in = arrived[BLOCK + 1 : BLOCK + 2, :].astype(jnp.int32) - 1
     for start in range(0, CELLS, 128):
@@ -256,7 +304,7 @@
     conduct = field[BLOCK : BLOCK + 1, :]
     row_ids = lax.broadcasted_iota(jnp.int32, (ROWS, CELLS), 0)
     source = jnp.where(row_ids < BLOCK, field, 0.0)
-    b_out[...] = source
+    b_ref[...] = source
 
     def operate(value, step):
         high, low = split2(jnp.where(row_ids == BLOCK, conduct, value))
@@ -285,7 +333,7 @@
                     halo_ssem.at[step, side], halo_rsem.at[step, side], peer,
                 )
             )
-            copies[-1].start()
+        start_both(*copies)
         forward(2 * FACE, 6 * FACE + ROWS)
         for face in range(2, 6):
             stack(face)
@@ -324,19 +372,18 @@
         local = [pair(dot_nn(fs_ref[face ^ 1], g_ref[face])) for face in range(2)]
         result = w_ref[:, 0:1] * value + conduct * f_ref[6 * FACE :, :] + backward(2, 6)
         for face in range(2):
-            copies[1 - face].wait_recv()
+            pl.when((has_left, has_right)[face])(copies[1 - face].wait_recv)
             high, low = split2(halo_recv[step, face])
             ghost = pair(dot_nn(jnp.concatenate([high, low], 0), gg_ref[face]))
             coefficients(face, local[face] + ghost)
         return result + backward(0, 2), copies
 
     image, copies_one = operate(source, 0)
-    y_out[...] = image
+    y_ref[...] = image
     second_image, copies_two = operate(image, 1)
-    z_out[...] = second_image
-
-    source = b_out[...]
-    image = y_out[...]
+
+    source = b_ref[...]
+    image = y_ref[...]
     lane = lax.broadcasted_iota(jnp.int32, (1, 128), 1)
     row = jnp.zeros((1, 128), F32)
     for index, terms in enumerate(
@@ -373,10 +420,15 @@
     grow = 1.0 + beta
     curvature = grow * (grow * by - alpha * (bz + yy)) + alpha * (alpha * yz)
     alpha_next = norm_next / curvature
-    coef_out[0:1, :] = jnp.broadcast_to(alpha + alpha_next * grow, (1, 128))
-    coef_out[1:2, :] = jnp.broadcast_to(alpha * alpha_next, (1, 128))
-    for one in [to_left, to_right] + copies_one + copies_two + sent:
+    first = alpha + alpha_next * grow
+    second = alpha * alpha_next
+    solution_out[...] = (first * source - second * image)[0:BLOCK]
+    residual_out[...] = (source - first * image + second * second_image)[0:BLOCK]
+    for one in sent:
         one.wait_send()
+    for one_left, one_right in ((to_left, to_right), copies_one, copies_two):
+        pl.when(has_left)(one_left.wait_send)
+        pl.when(has_right)(one_right.wait_send)
 
 
 def solution(mesh):
@@ -384,14 +436,23 @@
     x_size = min(X_SIZE, n_group)
     z_size = n_group // x_size
     constants = tables()
-    field = jax.ShapeDtypeStruct((ROWS, CELLS), F32)
     call = pl.pallas_call(
         functools.partial(kernel, n_curve, n_group, x_size),
-        out_shape=(field, field, field, jax.ShapeDtypeStruct((2, 128), F32)),
-        in_specs=[pl.BlockSpec(memory_space=pltpu.VMEM)] * 11,
-        out_specs=[pl.BlockSpec(memory_space=pltpu.VMEM)] * 4,
+        out_shape=(pltpu.VMEM((BLOCK, CELLS), F32), pltpu.VMEM((BLOCK, CELLS), F32)),
+        in_specs=[pl.BlockSpec(memory_space=pl.ANY)] * 11,
+        out_specs=[pl.BlockSpec(memory_space=pltpu.VMEM)] * 2,
         scratch_shapes=[
+            pltpu.VMEM((BLOCK, CELLS), F32),
+            pltpu.VMEM((1, CELLS), F32),
+            pltpu.VMEM((1, CELLS), jnp.int32),
+            pltpu.VMEM((6, CELLS), jnp.int32),
+            pltpu.VMEM((6, CELLS), jnp.int32),
+            pltpu.VMEM((2, GHOST), jnp.int32),
+            *[pltpu.VMEM(table.shape, table.dtype) for table in constants],
+            pltpu.SemaphoreType.DMA((11,)),
             pltpu.VMEM((ROWS, CELLS), F32),
+            pltpu.VMEM((ROWS, CELLS), F32),
+            pltpu.VMEM((16, CELLS), F32),
             pltpu.VMEM((3 * ROWS, CELLS), BF16),
             pltpu.VMEM((CELLS, CELLS), BF16),
             pltpu.VMEM((6, CELLS, CELLS), BF16),
@@ -425,13 +486,10 @@
     )
 
     def body(right_side, conductivity, destination, neighbour, orientation, send_list):
-        b, y, z, coef = call(
+        return call(
             right_side, conductivity[None], destination[None], neighbour, orientation, send_list,
             *[jnp.asarray(table) for table in constants],
         )
-        b, y, z = b[:BLOCK], y[:BLOCK], z[:BLOCK]
-        first, second = coef[0, 0], coef[1, 0]
-        return first * b - second * y, b - first * y + second * z
 
     in_specs = (
         P(None, CURVE_GROUP),

time: 58.6 us -> 53.9 us (0.920)
  other arithmetic: 3.23 us -> 0 us
  Pallas kernels: 53.3 us -> 51.6 us
    add x1 -> x0, other arithmetic: 3.23 us -> none  [body(): return (first * b - second * y, b - first * y + second * z)]
    pallas_call x1, Pallas kernels: 53.3 us -> 51.6 us  [body(): call(right_side, conductivity[None], destination[None], neighbour, orient...]
    unnamed x2, local copies, waits for them, and re-layouts: 0.63 us -> 1.41 us
where the time goes in v2:
time: 53.9 us; the launch traced here: 53.7 us
  Pallas kernels  51.6 us (96%)
  local copies, waits for them, and re-layouts  1.41 us (3%)
  between operations  0.64 us (1%)
    pallas_call x1, Pallas kernels, body(): call(right_side, conductivity[None], destination[None], neighbour, orient...  51.6 us
    unnamed x2, local copies, waits for them, and re-layouts  1.41 us

profile of v2, /device:TPU:2, one launch (start us, length us, event | category | flops | bytes accessed | tf_op | source)
XLA Modules:
  0.0 53.7 jit_solution(15914359918925129368)
XLA Ops:
  0.6 51.6 %shard_map.122 = (f32[125,512]{1,0:T(8,128)S(1)}, f32[125,512]{1,0:T(8,128)S(1)}) custom-call(f32[125,512]{1,0:T(8,128)} %rs_hbm.1, f32[1,512]{1,0:T(1,128)} %bitcast.2, s32[1,512]{1,0:T(1,128)} %bitcast.3, s32[6,512]{1,0:T(8,128)} %nb_hbm.1, s32[6,512]{1,0:T(8,128)} %ori_hbm.1, s32[2,256]{1,0:T(2,128)} %sl_hbm.1, bf16[512,256]{1,0:T(8,128)(2,1)} %constant.10.clone.fa_hbm, ...), custom_call_target="tpu_custom_call" | custom-call | tf_op jit(solution)/shard_map/pallas_call | solution.py:489
  52.3 0.7 %copy.15 = f32[125,512]{1,0:T(8,128)} copy(f32[125,512]{1,0:T(8,128)S(1)} %get-tuple-element.2) | data formatting | bytes 512000
  53.0 0.7 %copy.16 = f32[125,512]{1,0:T(8,128)} copy(f32[125,512]{1,0:T(8,128)S(1)} %get-tuple-element.3) | data formatting | bytes 512000

commit v3 on v2

--- a/solution.py
+++ b/solution.py
@@ -143,6 +143,12 @@
     return high, mid, (rest - mid.astype(F32)).astype(BF16)
 
 
+def far_first(sizes):
+    offsets = [tuple(int(i) for i in index) for index in np.ndindex(*sizes) if any(index)]
+    offsets.sort(key=lambda index: -sum(min(i, n - i) for i, n in zip(index, sizes)))
+    return [index[0] if len(sizes) == 1 else index for index in offsets]
+
+
 def onehot(index_row, rows, start=0):
     ids = lax.broadcasted_iota(jnp.int32, (rows, index_row.shape[1]), 0) + start
     return jnp.where(ids == index_row, 1.0, 0.0).astype(BF16)
@@ -154,8 +160,8 @@
     solution_out, residual_out,
     rs_ref, cond_ref, dest_ref, nb_ref, ori_ref, sl_ref, fa_ref, fb_ref, bh_ref, bl_ref, w_ref, load_sem,
     b_ref, y_ref, tail_ref, x3_ref, q_ref, g_ref, gg_ref, s_ref, sign_ref, f_ref, fs_ref, ch_ref, cl_ref,
-    mig_send, mig_recv, halo_send, halo_recv, row_send, curve_recv, x_recv, z_recv,
-    mig_ssem, mig_rsem, halo_ssem, halo_rsem, curve_ssem, curve_rsem, x_ssem, x_rsem, z_ssem, z_rsem,
+    mig_send, mig_recv, halo_send, halo_recv, row_send, curve_recv, group_recv,
+    mig_ssem, mig_rsem, halo_ssem, halo_rsem, curve_ssem, curve_rsem, group_ssem, group_rsem,
 ):
     curve = lax.axis_index("curve")
     group = lax.axis_index("group")
@@ -170,22 +176,12 @@
     z_size = n_group // x_size
     x_pos = lax.rem(group, x_size)
     z_pos = group // x_size
-    curve_peers = [(lax.rem(curve + d, n_curve), group) for d in range(1, n_curve)]
-    x_peers = [(curve, z_pos * x_size + lax.rem(x_pos + d, x_size)) for d in range(1, x_size)]
-    z_peers = [(curve, lax.rem(z_pos + d, z_size) * x_size + x_pos) for d in range(1, z_size)]
-    everyone = curve_peers + x_peers + z_peers
-
-    barrier = pltpu.get_barrier_semaphore()
-    for peer in everyone:
-        pl.semaphore_signal(barrier, inc=1, device_id=peer, device_id_type=MESH)
-
-    @pl.when(has_left)
-    def _():
-        pl.semaphore_signal(barrier, inc=1, device_id=left, device_id_type=MESH)
-
-    @pl.when(has_right)
-    def _():
-        pl.semaphore_signal(barrier, inc=1, device_id=right, device_id_type=MESH)
+    curve_peers = [(lax.rem(curve + d, n_curve), group) for d in far_first((n_curve,))]
+    group_peers = [
+        (curve, lax.rem(z_pos + dz, z_size) * x_size + lax.rem(x_pos + dx, x_size))
+        for dz, dx in far_first((z_size, x_size))
+    ]
+    everyone = curve_peers + group_peers
 
     loads = {}
     for i, (name, source, sink) in enumerate(
@@ -205,6 +201,18 @@
     ):
         loads[name] = pltpu.make_async_copy(source, sink, load_sem.at[i])
         loads[name].start()
+    barrier = pltpu.get_barrier_semaphore()
+    for peer in everyone:
+        pl.semaphore_signal(barrier, inc=1, device_id=peer, device_id_type=MESH)
+
+    @pl.when(has_left)
+    def _():
+        pl.semaphore_signal(barrier, inc=1, device_id=left, device_id_type=MESH)
+
+    @pl.when(has_right)
+    def _():
+        pl.semaphore_signal(barrier, inc=1, device_id=right, device_id_type=MESH)
+
     for start in range(0, CELLS, 64):
         ids = lax.broadcasted_iota(jnp.int32, (64, CELLS), 0) + start
         lanes = lax.broadcasted_iota(jnp.int32, (64, CELLS), 1)
@@ -395,8 +403,7 @@
     for phase, (peers, landing, ssem, rsem) in enumerate(
         (
             (curve_peers, curve_recv, curve_ssem, curve_rsem),
-            (x_peers, x_recv, x_ssem, x_rsem),
-            (z_peers, z_recv, z_ssem, z_rsem),
+            (group_peers, group_recv, group_ssem, group_rsem),
         )
     ):
         row_send[phase] = row
@@ -406,9 +413,12 @@
         ]
         for one in out:
             one.start()
-        for i, one in enumerate(out):
+        for one in out:
             one.wait_recv()
-            row = row + landing[i]
+        terms = [row] + [landing[i] for i in range(len(out))]
+        while len(terms) > 1:
+            terms = [sum(terms[i + 1 : i + 2], terms[i]) for i in range(0, len(terms), 2)]
+        row = terms[0]
         sent += out
 
     bb, by, yy, bz, yz = (
@@ -431,10 +441,20 @@
         pl.when(has_right)(one_right.wait_send)
 
 
+def write_kernel(solution_ref, residual_ref, solution_out, residual_out, sem):
+    copies = [
+        pltpu.make_async_copy(solution_ref, solution_out, sem.at[0]),
+        pltpu.make_async_copy(residual_ref, residual_out, sem.at[1]),
+    ]
+    for one in copies:
+        one.start()
+    for one in copies:
+        one.wait()
+
+
 def solution(mesh):
     n_curve, n_group = mesh.shape["curve"], mesh.shape["group"]
     x_size = min(X_SIZE, n_group)
-    z_size = n_group // x_size
     constants = tables()
     call = pl.pallas_call(
         functools.partial(kernel, n_curve, n_group, x_size),
@@ -467,29 +487,36 @@
             pltpu.VMEM((2 * MOVE, ROWS), F32),
             pltpu.VMEM((2, 2, FACE, GHOST), F32),
             pltpu.VMEM((2, 2, FACE, GHOST), F32),
-            pltpu.VMEM((3, 1, 128), F32),
+            pltpu.VMEM((2, 1, 128), F32),
             pltpu.VMEM((n_curve - 1, 1, 128), F32),
-            pltpu.VMEM((x_size - 1, 1, 128), F32),
-            pltpu.VMEM((z_size - 1, 1, 128), F32),
+            pltpu.VMEM((n_group - 1, 1, 128), F32),
             pltpu.SemaphoreType.DMA((2,)),
             pltpu.SemaphoreType.DMA((2,)),
             pltpu.SemaphoreType.DMA((2, 2)),
             pltpu.SemaphoreType.DMA((2, 2)),
             pltpu.SemaphoreType.DMA((n_curve - 1,)),
             pltpu.SemaphoreType.DMA((n_curve - 1,)),
-            pltpu.SemaphoreType.DMA((x_size - 1,)),
-            pltpu.SemaphoreType.DMA((x_size - 1,)),
-            pltpu.SemaphoreType.DMA((z_size - 1,)),
-            pltpu.SemaphoreType.DMA((z_size - 1,)),
+            pltpu.SemaphoreType.DMA((n_group - 1,)),
+            pltpu.SemaphoreType.DMA((n_group - 1,)),
         ],
         compiler_params=pltpu.CompilerParams(collective_id=0, has_side_effects=True),
     )
 
+    field = jax.ShapeDtypeStruct((BLOCK, CELLS), F32)
+    write = pl.pallas_call(
+        write_kernel,
+        out_shape=(field, field),
+        in_specs=[pl.BlockSpec(memory_space=pltpu.VMEM)] * 2,
+        out_specs=[pl.BlockSpec(memory_space=pl.ANY)] * 2,
+        scratch_shapes=[pltpu.SemaphoreType.DMA((2,))],
+    )
+
     def body(right_side, conductivity, destination, neighbour, orientation, send_list):
-        return call(
+        fields = call(
             right_side, conductivity[None], destination[None], neighbour, orientation, send_list,
             *[jnp.asarray(table) for table in constants],
         )
+        return write(*[pltpu.with_memory_space_constraint(one, pltpu.VMEM) for one in fields])
 
     in_specs = (
         P(None, CURVE_GROUP),

time: 53.9 us -> 54.9 us (1.019)
  the two profiles are of different devices: /device:TPU:2 before, /device:TPU:1 now
where the time goes in v3:
time: 54.9 us; the launch traced here: 54.7 us
  Pallas kernels  54.1 us (99%)
  between operations  0.64 us (1%)
    pallas_call x1, Pallas kernels, body(): call(right_side, conductivity[None], destination[None], neighbour, orient...  53.3 us

profile of v3, /device:TPU:1, one launch (start us, length us, event | category | flops | bytes accessed | tf_op | source)
XLA Modules:
  0.0 54.7 jit_solution(7947482631799246952)
XLA Ops:
  0.6 53.3 %shard_map.122 = (f32[125,512]{1,0:T(8,128)S(1)}, f32[125,512]{1,0:T(8,128)S(1)}) custom-call(f32[125,512]{1,0:T(8,128)} %rs_hbm.1, f32[1,512]{1,0:T(1,128)} %bitcast.2, s32[1,512]{1,0:T(1,128)} %bitcast.3, s32[6,512]{1,0:T(8,128)} %nb_hbm.1, s32[6,512]{1,0:T(8,128)} %ori_hbm.1, s32[2,256]{1,0:T(2,128)} %sl_hbm.1, bf16[512,256]{1,0:T(8,128)(2,1)} %constant.10.clone.fa_hbm, ...), custom_call_target="tpu_custom_call" | custom-call | tf_op jit(solution)/shard_map/pallas_call | solution.py:515
  53.9 0.8 %shard_map.123 = (f32[125,512]{1,0:T(8,128)}, f32[125,512]{1,0:T(8,128)}) custom-call(f32[125,512]{1,0:T(8,128)S(1)} %get-tuple-element.4.solution_ref, f32[125,512]{1,0:T(8,128)S(1)} %get-tuple-element.5.residual_ref), custom_call_target="tpu_custom_call" | custom-call | tf_op jit(solution)/shard_map/pallas_call | solution.py:519

commit v4 on v3

--- a/solution.py
+++ b/solution.py
@@ -115,10 +115,7 @@
     fwd_high, fwd_low = halves(forward)
     back_high, back_low = halves(backward)
     return (
-        np.concatenate([fwd_high, fwd_high], 1),
-        fwd_low,
-        back_high,
-        back_low,
+        np.concatenate([np.concatenate([fwd_high, fwd_high, fwd_low], 1), back_high, back_low], 0),
         np.broadcast_to(weight_rows, (ROWS, 128)).astype(np.float32),
     )
 
@@ -156,12 +153,12 @@
 
 def kernel(
     n_curve, n_group, x_size,
-    rs_hbm, cond_hbm, dest_hbm, nb_hbm, ori_hbm, sl_hbm, fa_hbm, fb_hbm, bh_hbm, bl_hbm, w_hbm,
+    rs_hbm, cond_hbm, dest_hbm, nb_hbm, ori_hbm, sl_hbm, table_hbm, w_hbm,
     solution_out, residual_out,
-    rs_ref, cond_ref, dest_ref, nb_ref, ori_ref, sl_ref, fa_ref, fb_ref, bh_ref, bl_ref, w_ref, load_sem,
+    rs_ref, cond_ref, dest_ref, nb_ref, ori_ref, sl_ref, table_ref, w_ref, load_sem,
     b_ref, y_ref, tail_ref, x3_ref, q_ref, g_ref, gg_ref, s_ref, sign_ref, f_ref, fs_ref, ch_ref, cl_ref,
     mig_send, mig_recv, halo_send, halo_recv, row_send, curve_recv, group_recv,
-    mig_ssem, mig_rsem, halo_ssem, halo_rsem, curve_ssem, curve_rsem, group_ssem, group_rsem,
+    mig_ssem, mig_rsem, halo_ssem, halo_rsem, curve_ssem, curve_rsem, group_ssem, group_rsem, one_sem, two_sem, plane_sem,
 ):
     curve = lax.axis_index("curve")
     group = lax.axis_index("group")
@@ -181,7 +178,50 @@
         (curve, lax.rem(z_pos + dz, z_size) * x_size + lax.rem(x_pos + dx, x_size))
         for dz, dx in far_first((z_size, x_size))
     ]
-    everyone = curve_peers + group_peers
+    y_size = n_curve // 2
+    core = lax.rem(curve, 2)
+    core_peer = (curve + 1 - 2 * core, group)
+
+    def along(dim, offset):
+        if dim == 0:
+            return (curve, z_pos * x_size + lax.rem(x_pos + offset, x_size))
+        if dim == 1:
+            return (lax.rem(curve + 2 * offset, n_curve), group)
+        return (curve, lax.rem(z_pos + offset, z_size) * x_size + x_pos)
+
+    sizes = (x_size, y_size, z_size)
+    near_peers = [core_peer] + [
+        along(dim, offset) for dim in range(3) for offset in sorted({1, sizes[dim] - 1}) if sizes[dim] > 1
+    ]
+
+    def signal(sem, peer):
+        pl.semaphore_signal(sem, inc=1, device_id=peer, device_id_type=MESH)
+
+    def spread(reach, ring_sem):
+        for dim in range(3):
+            if sizes[dim] > 2 * reach + 1:
+                signal(ring_sem.at[dim], along(dim, reach))
+                signal(ring_sem.at[dim], along(dim, sizes[dim] - reach))
+
+    def gather_known(reach, ring_sem):
+        for dim in range(3):
+            if sizes[dim] > 2 * reach + 1:
+                pl.semaphore_wait(ring_sem.at[dim], 2)
+
+    def after_moves():
+        gather_known(1, one_sem)
+        spread(2, two_sem)
+
+    def after_first():
+        gather_known(2, two_sem)
+        signal(plane_sem.at[0], core_peer)
+        for offset in range(1, x_size):
+            signal(plane_sem.at[1], along(0, offset))
+
+    def before_sums():
+        pl.semaphore_wait(plane_sem.at[0], 1)
+        if x_size > 1:
+            pl.semaphore_wait(plane_sem.at[1], x_size - 1)
 
     loads = {}
     for i, (name, source, sink) in enumerate(
@@ -192,26 +232,23 @@
             ("nb", nb_hbm, nb_ref),
             ("sl", sl_hbm, sl_ref),
             ("ori", ori_hbm, ori_ref),
-            ("fa", fa_hbm, fa_ref),
-            ("fb", fb_hbm, fb_ref),
-            ("bh", bh_hbm, bh_ref),
-            ("bl", bl_hbm, bl_ref),
+            ("table", table_hbm, table_ref),
             ("w", w_hbm, w_ref),
         )
     ):
         loads[name] = pltpu.make_async_copy(source, sink, load_sem.at[i])
         loads[name].start()
     barrier = pltpu.get_barrier_semaphore()
-    for peer in everyone:
-        pl.semaphore_signal(barrier, inc=1, device_id=peer, device_id_type=MESH)
+    for peer in near_peers:
+        signal(barrier, peer)
 
     @pl.when(has_left)
     def _():
-        pl.semaphore_signal(barrier, inc=1, device_id=left, device_id_type=MESH)
+        signal(barrier, left)
 
     @pl.when(has_right)
     def _():
-        pl.semaphore_signal(barrier, inc=1, device_id=right, device_id_type=MESH)
+        signal(barrier, right)
 
     for start in range(0, CELLS, 64):
         ids = lax.broadcasted_iota(jnp.int32, (64, CELLS), 0) + start
@@ -249,7 +286,7 @@
     packed = dot_nt(onehot(place, 2 * MOVE), x3_ref[...])
     mig_send[...] = packed[:, 0:ROWS] + packed[:, ROWS : 2 * ROWS] + packed[:, 2 * ROWS :]
 
-    pl.semaphore_wait(barrier, len(everyone) + has_left.astype(jnp.int32) + has_right.astype(jnp.int32))
+    pl.semaphore_wait(barrier, len(near_peers) + has_left.astype(jnp.int32) + has_right.astype(jnp.int32))
 
     def copy(source, sink, ssem, rsem, peer):
         return pltpu.make_async_remote_copy(
@@ -267,6 +304,7 @@
         mig_send.at[pl.ds(MOVE, MOVE)], mig_recv.at[pl.ds(0, MOVE)], mig_ssem.at[1], mig_rsem.at[1], right
     )
     start_both(to_left, to_right)
+    spread(1, one_sem)
     loads["nb"].wait()
     loads["sl"].wait()
     loads["ori"].wait()
@@ -298,8 +336,8 @@
         second_bit = lax.shift_right_arithmetic(code, 1).astype(F32)
         sign_ref[face] = (1.0 - odd_first * first_bit) * (1.0 - odd_second * second_bit)
 
-    for name in ("fa", "fb", "bh", "bl", "w"):
-        loads[name].wait()
+    loads["table"].wait()
+    loads["w"].wait()
     pl.when(has_left)(to_right.wait_recv)
     pl.when(has_right)(to_left.wait_recv)
     arrived = mig_recv[...].T
@@ -320,7 +358,7 @@
 
         def forward(start, stop):
             rows = pl.ds(start, stop - start)
-            f_ref[rows, :] = dot_nn(fa_ref[rows, :], both) + dot_nn(fb_ref[rows, :], high)
+            f_ref[rows, :] = dot_nn(table_ref[rows, 0:256], both) + dot_nn(table_ref[rows, 256:384], high)
 
         def stack(face):
             high, low = split2(f_ref[face * FACE : (face + 1) * FACE, :])
@@ -368,17 +406,18 @@
 
         def backward(start, stop):
             columns = slice(start * FACE, stop * FACE)
-            back_high = bh_ref[:, columns]
+            back_high = table_ref[512:640, columns]
             return (
                 dot_nn(back_high, ch_ref[columns, :])
                 + dot_nn(back_high, cl_ref[columns, :])
-                + dot_nn(bl_ref[:, columns], ch_ref[columns, :])
+                + dot_nn(table_ref[640:768, columns], ch_ref[columns, :])
             )
 
         for face in range(2, 6):
             coefficients(face, pair(dot_nn(fs_ref[face ^ 1], g_ref[face])))
         local = [pair(dot_nn(fs_ref[face ^ 1], g_ref[face])) for face in range(2)]
         result = w_ref[:, 0:1] * value + conduct * f_ref[6 * FACE :, :] + backward(2, 6)
+        (after_moves, after_first)[step]()
         for face in range(2):
             pl.when((has_left, has_right)[face])(copies[1 - face].wait_recv)
             high, low = split2(halo_recv[step, face])
@@ -399,6 +438,7 @@
     ):
         row = row + jnp.where(lane == index, jnp.sum(terms, axis=(0, 1), keepdims=True), 0.0)
 
+    before_sums()
     sent = []
     for phase, (peers, landing, ssem, rsem) in enumerate(
         (
@@ -407,19 +447,15 @@
         )
     ):
         row_send[phase] = row
-        out = [
-            copy(row_send.at[phase], landing.at[i], ssem.at[i], rsem.at[i], peer)
-            for i, peer in enumerate(peers)
-        ]
-        for one in out:
-            one.start()
-        for one in out:
-            one.wait_recv()
-        terms = [row] + [landing[i] for i in range(len(out))]
+        for i, peer in enumerate(peers):
+            copy(row_send.at[phase], landing.at[i], ssem, rsem, peer).start()
+        every = copy(landing, landing, ssem, rsem, peers[0])
+        every.wait_recv()
+        terms = [row] + [landing[i] for i in range(len(peers))]
         while len(terms) > 1:
             terms = [sum(terms[i + 1 : i + 2], terms[i]) for i in range(0, len(terms), 2)]
         row = terms[0]
-        sent += out
+        sent.append(every)
 
     bb, by, yy, bz, yz = (
         jnp.sum(jnp.where(lane == index, row, 0.0), axis=1, keepdims=True) for index in range(5)
@@ -459,7 +495,7 @@
     call = pl.pallas_call(
         functools.partial(kernel, n_curve, n_group, x_size),
         out_shape=(pltpu.VMEM((BLOCK, CELLS), F32), pltpu.VMEM((BLOCK, CELLS), F32)),
-        in_specs=[pl.BlockSpec(memory_space=pl.ANY)] * 11,
+        in_specs=[pl.BlockSpec(memory_space=pl.ANY)] * 8,
         out_specs=[pl.BlockSpec(memory_space=pltpu.VMEM)] * 2,
         scratch_shapes=[
             pltpu.VMEM((BLOCK, CELLS), F32),
@@ -469,7 +505,7 @@
             pltpu.VMEM((6, CELLS), jnp.int32),
             pltpu.VMEM((2, GHOST), jnp.int32),
             *[pltpu.VMEM(table.shape, table.dtype) for table in constants],
-            pltpu.SemaphoreType.DMA((11,)),
+            pltpu.SemaphoreType.DMA((8,)),
             pltpu.VMEM((ROWS, CELLS), F32),
             pltpu.VMEM((ROWS, CELLS), F32),
             pltpu.VMEM((16, CELLS), F32),
@@ -494,10 +530,13 @@
             pltpu.SemaphoreType.DMA((2,)),
             pltpu.SemaphoreType.DMA((2, 2)),
             pltpu.SemaphoreType.DMA((2, 2)),
-            pltpu.SemaphoreType.DMA((n_curve - 1,)),
-            pltpu.SemaphoreType.DMA((n_curve - 1,)),
-            pltpu.SemaphoreType.DMA((n_group - 1,)),
-            pltpu.SemaphoreType.DMA((n_group - 1,)),
+            pltpu.SemaphoreType.DMA,
+            pltpu.SemaphoreType.DMA,
+            pltpu.SemaphoreType.DMA,
+            pltpu.SemaphoreType.DMA,
+            pltpu.SemaphoreType.REGULAR((3,)),
+            pltpu.SemaphoreType.REGULAR((3,)),
+            pltpu.SemaphoreType.REGULAR((2,)),
         ],
         compiler_params=pltpu.CompilerParams(collective_id=0, has_side_effects=True),
     )

time: 54.9 us -> 50.5 us (0.920)
  Pallas kernels: 54.1 us -> 49.7 us
    pallas_call x1, Pallas kernels: 53.3 us -> 48.9 us  [body(): call(right_side, conductivity[None], destination[None], neighbour, orient...]
where the time goes in v4:
time: 50.5 us; the launch traced here: 50.4 us
  Pallas kernels  49.7 us (98%)
  between operations  0.64 us (1%)
    pallas_call x1, Pallas kernels, body(): call(right_side, conductivity[None], destination[None], neighbour, orient...  48.9 us

profile of v4, /device:TPU:1, one launch (start us, length us, event | category | flops | bytes accessed | tf_op | source)
XLA Modules:
  0.0 50.4 jit_solution(9503015148074383108)
XLA Ops:
  0.6 48.9 %shard_map.95 = (f32[125,512]{1,0:T(8,128)S(1)}, f32[125,512]{1,0:T(8,128)S(1)}) custom-call(f32[125,512]{1,0:T(8,128)} %rs_hbm.1, f32[1,512]{1,0:T(1,128)} %bitcast.2, s32[1,512]{1,0:T(1,128)} %bitcast.3, s32[6,512]{1,0:T(8,128)} %nb_hbm.1, s32[6,512]{1,0:T(8,128)} %ori_hbm.1, s32[2,256]{1,0:T(2,128)} %sl_hbm.1, bf16[768,384]{1,0:T(8,128)(2,1)} %constant.4.clone.table_hbm, ...), custom_call_target="tpu_custom_call" | custom-call | tf_op jit(solution)/shard_map/pallas_call | solution.py:554
  49.6 0.8 %shard_map.96 = (f32[125,512]{1,0:T(8,128)}, f32[125,512]{1,0:T(8,128)}) custom-call(f32[125,512]{1,0:T(8,128)S(1)} %get-tuple-element.4.solution_ref, f32[125,512]{1,0:T(8,128)S(1)} %get-tuple-element.5.residual_ref), custom_call_target="tpu_custom_call" | custom-call | tf_op jit(solution)/shard_map/pallas_call | solution.py:558

commit v5 on v4

--- a/solution.py
+++ b/solution.py
@@ -105,18 +105,22 @@
         backward[:BLOCK, row : row + 25] = trace.T * mode_weight
         backward[:BLOCK, row + HALF : row + HALF + 25] = -0.5 * normal.T * mode_weight
     forward[6 * FACE : 6 * FACE + BLOCK, :BLOCK] = volume
-    weight_rows = np.zeros((ROWS, 1))
+    face_rows = np.zeros(HALF)
+    face_rows[:25] = mode_weight
+    weight_rows = np.zeros((ROWS, 128))
     weight_rows[:BLOCK, 0] = cell_weight
 
     def halves(table):
         high = table.astype(ml_dtypes.bfloat16)
         return high, (table - high.astype(np.float64)).astype(ml_dtypes.bfloat16)
 
+    weight_rows[: 2 * FACE, 1] = np.tile(np.concatenate([face_rows, -0.5 * face_rows]), 2)
     fwd_high, fwd_low = halves(forward)
     back_high, back_low = halves(backward)
+    again = np.concatenate(halves(forward[: 2 * FACE] @ backward[:, : 2 * FACE]) + (np.zeros((ROWS, ROWS), ml_dtypes.bfloat16),), 1)
     return (
-        np.concatenate([np.concatenate([fwd_high, fwd_high, fwd_low], 1), back_high, back_low], 0),
-        np.broadcast_to(weight_rows, (ROWS, 128)).astype(np.float32),
+        np.concatenate([np.concatenate([fwd_high, fwd_high, fwd_low], 1), back_high, back_low, again], 0),
+        weight_rows.astype(np.float32),
     )
 
 
@@ -156,7 +160,7 @@
     rs_hbm, cond_hbm, dest_hbm, nb_hbm, ori_hbm, sl_hbm, table_hbm, w_hbm,
     solution_out, residual_out,
     rs_ref, cond_ref, dest_ref, nb_ref, ori_ref, sl_ref, table_ref, w_ref, load_sem,
-    b_ref, y_ref, tail_ref, x3_ref, q_ref, g_ref, gg_ref, s_ref, sign_ref, f_ref, fs_ref, ch_ref, cl_ref,
+    b_ref, y_ref, z_ref, fb_ref, tail_ref, x3_ref, q_ref, g_ref, gg_ref, s_ref, sign_ref, f_ref, fs_ref, ch_ref, cl_ref,
     mig_send, mig_recv, halo_send, halo_recv, row_send, curve_recv, group_recv,
     mig_ssem, mig_rsem, halo_ssem, halo_rsem, curve_ssem, curve_rsem, group_ssem, group_rsem, one_sem, two_sem, plane_sem,
 ):
@@ -208,11 +212,11 @@
             if sizes[dim] > 2 * reach + 1:
                 pl.semaphore_wait(ring_sem.at[dim], 2)
 
-    def after_moves():
+    def two_away():
         gather_known(1, one_sem)
         spread(2, two_sem)
 
-    def after_first():
+    def whole_plane():
         gather_known(2, two_sem)
         signal(plane_sem.at[0], core_peer)
         for offset in range(1, x_size):
@@ -222,6 +226,16 @@
         pl.semaphore_wait(plane_sem.at[0], 1)
         if x_size > 1:
             pl.semaphore_wait(plane_sem.at[1], x_size - 1)
+
+    barrier = pltpu.get_barrier_semaphore()
+
+    @pl.when(has_left)
+    def _():
+        signal(barrier, left)
+
+    @pl.when(has_right)
+    def _():
+        signal(barrier, right)
 
     loads = {}
     for i, (name, source, sink) in enumerate(
@@ -238,17 +252,8 @@
     ):
         loads[name] = pltpu.make_async_copy(source, sink, load_sem.at[i])
         loads[name].start()
-    barrier = pltpu.get_barrier_semaphore()
     for peer in near_peers:
         signal(barrier, peer)
-
-    @pl.when(has_left)
-    def _():
-        signal(barrier, left)
-
-    @pl.when(has_right)
-    def _():
-        signal(barrier, right)
 
     for start in range(0, CELLS, 64):
         ids = lax.broadcasted_iota(jnp.int32, (64, CELLS), 0) + start
@@ -309,15 +314,43 @@
     loads["sl"].wait()
     loads["ori"].wait()
 
+    def project(field, rows=slice(0, 2 * FACE)):
+        high, low = field
+        return dot_nn(table_ref[rows, 0:256], jnp.concatenate([high, low], 0)) + dot_nn(
+            table_ref[rows, 256:384], high
+        )
+
+    def stack(face):
+        high, low = split2(f_ref[face * FACE : (face + 1) * FACE, :])
+        fs_ref[face, 0:FACE, :] = high
+        fs_ref[face, FACE : 2 * FACE, :] = low
+
+    def pair(product):
+        return product[0:FACE] + product[FACE : 2 * FACE]
+
+    def halo(step):
+        return [
+            copy(
+                halo_send.at[step, side], halo_recv.at[step, 1 - side],
+                halo_ssem.at[step, side], halo_rsem.at[step, side], peer,
+            )
+            for side, peer in ((0, left), (1, right))
+        ]
+
     staying = jnp.where(target == 0, slot, -1)
     for start in range(0, CELLS, 64):
         q_ref[start : start + 64, :] = onehot(staying, 64, start)
     stay = dot_nt(x3_ref[...], q_ref[...])
-    f_ref[0:ROWS, :] = stay[0:ROWS] + stay[ROWS : 2 * ROWS] + stay[2 * ROWS :]
-
+    y_ref[...] = stay[0:ROWS] + stay[ROWS : 2 * ROWS] + stay[2 * ROWS :]
     for side in range(2):
         for start in range(0, CELLS, 128):
             s_ref[side, start : start + 128, :] = onehot(sl_ref[side : side + 1, :], 128, start)
+    loads["table"].wait()
+    loads["w"].wait()
+    f_ref[0 : 2 * FACE, :] = project(split2(y_ref[...]))
+    for side in range(2):
+        stack(side)
+        halo_send[0, side] = pair(dot_nn(fs_ref[side], s_ref[side]))
     mode = lax.broadcasted_iota(jnp.int32, (HALF, CELLS), 0)
     odd_first = jnp.where((mode >= 15) & (mode < 25), 2.0, 0.0)
     second = functools.reduce(jnp.logical_or, [mode == 5 * i + j for i in range(5) for j in (3, 4)])
@@ -336,107 +369,118 @@
         second_bit = lax.shift_right_arithmetic(code, 1).astype(F32)
         sign_ref[face] = (1.0 - odd_first * first_bit) * (1.0 - odd_second * second_bit)
 
-    loads["table"].wait()
-    loads["w"].wait()
+    two_away()
     pl.when(has_left)(to_right.wait_recv)
     pl.when(has_right)(to_left.wait_recv)
+
     arrived = mig_recv[...].T
+    slot_in = mig_recv[:, BLOCK + 1 : BLOCK + 2].astype(jnp.int32) - 1
+    faces = project(split2(arrived))
+    for side in range(2):
+        listed = jnp.where(slot_in == sl_ref[side : side + 1, :], 1.0, 0.0).astype(BF16)
+        parts = jnp.concatenate(split2(faces[side * FACE : (side + 1) * FACE]), 0)
+        halo_send[0, side] += pair(dot_nn(parts, listed))
+    copies_one = halo(0)
+    start_both(*copies_one)
+
     place_in = arrived[BLOCK + 1 : BLOCK + 2, :].astype(jnp.int32) - 1
     for start in range(0, CELLS, 128):
         q_ref[start : start + 128, 0 : 2 * MOVE] = onehot(place_in, 128, start)
-    parts = jnp.concatenate(split3(arrived), 0)
-    moved = dot_nt(parts, q_ref[:, 0 : 2 * MOVE])
-    field = f_ref[0:ROWS, :] + (moved[0:ROWS] + moved[ROWS : 2 * ROWS] + moved[2 * ROWS :])
+    moved = dot_nt(jnp.concatenate(split3(arrived), 0), q_ref[:, 0 : 2 * MOVE])
+    field = y_ref[...] + (moved[0:ROWS] + moved[ROWS : 2 * ROWS] + moved[2 * ROWS :])
     conduct = field[BLOCK : BLOCK + 1, :]
     row_ids = lax.broadcasted_iota(jnp.int32, (ROWS, CELLS), 0)
-    source = jnp.where(row_ids < BLOCK, field, 0.0)
-    b_ref[...] = source
-
-    def operate(value, step):
-        high, low = split2(jnp.where(row_ids == BLOCK, conduct, value))
-        both = jnp.concatenate([high, low], 0)
-
-        def forward(start, stop):
-            rows = pl.ds(start, stop - start)
-            f_ref[rows, :] = dot_nn(table_ref[rows, 0:256], both) + dot_nn(table_ref[rows, 256:384], high)
-
-        def stack(face):
-            high, low = split2(f_ref[face * FACE : (face + 1) * FACE, :])
-            fs_ref[face, 0:FACE, :] = high
-            fs_ref[face, FACE : 2 * FACE, :] = low
-
-        def pair(product):
-            return product[0:FACE] + product[FACE : 2 * FACE]
-
-        copies = []
-        forward(0, 2 * FACE)
-        for side, peer in ((0, left), (1, right)):
-            stack(side)
-            halo_send[step, side] = pair(dot_nn(fs_ref[side], s_ref[side]))
-            copies.append(
-                copy(
-                    halo_send.at[step, side], halo_recv.at[step, 1 - side],
-                    halo_ssem.at[step, side], halo_rsem.at[step, side], peer,
-                )
-            )
-        start_both(*copies)
-        forward(2 * FACE, 6 * FACE + ROWS)
+    b_ref[...] = jnp.where(row_ids < BLOCK, field, 0.0)
+
+    def with_conduct(value):
+        return jnp.where(row_ids == BLOCK, conduct, value)
+
+    def coefficients(face, near):
+        row = face * FACE
+        trace = f_ref[row : row + HALF, :]
+        normal = f_ref[row + HALF : row + FACE, :]
+        near_conduct = near[25:26, :]
+        sign = sign_ref[face]
+        near_value = sign * near[0:HALF]
+        near_normal = sign * near[HALF:FACE]
+        penalty = PENALTY * jnp.maximum(conduct, near_conduct)
+        jump = outside[face] * trace - near_value
+        first = (
+            penalty * jump - (0.5 * outside[face] * conduct) * normal + (0.5 * near_conduct) * near_normal
+        )
+        parts = (first, conduct * jump)
+        for offset, part in zip((0, HALF), parts):
+            high, low = split2(part)
+            ch_ref[row + offset : row + offset + HALF, :] = high
+            cl_ref[row + offset : row + offset + HALF, :] = low
+        return parts
+
+    def expand(high, low, columns):
+        return (
+            dot_nn(high, ch_ref[columns, :])
+            + dot_nn(high, cl_ref[columns, :])
+            + dot_nn(low, ch_ref[columns, :])
+        )
+
+    def backward(start, stop):
+        columns = slice(start * FACE, stop * FACE)
+        return expand(table_ref[512:640, columns], table_ref[640:768, columns], columns)
+
+    def local_part(value_ref, result_ref):
         for face in range(2, 6):
             stack(face)
-
-        def coefficients(face, near):
-            row = face * FACE
-            trace = f_ref[row : row + HALF, :]
-            normal = f_ref[row + HALF : row + FACE, :]
-            near_conduct = near[25:26, :]
-            sign = sign_ref[face]
-            near_value = sign * near[0:HALF]
-            near_normal = sign * near[HALF:FACE]
-            penalty = PENALTY * jnp.maximum(conduct, near_conduct)
-            jump = outside[face] * trace - near_value
-            first = (
-                penalty * jump
-                - (0.5 * outside[face] * conduct) * normal
-                + (0.5 * near_conduct) * near_normal
-            )
-            for offset, part in ((0, first), (HALF, conduct * jump)):
-                high, low = split2(part)
-                ch_ref[row + offset : row + offset + HALF, :] = high
-                cl_ref[row + offset : row + offset + HALF, :] = low
-
-        def backward(start, stop):
-            columns = slice(start * FACE, stop * FACE)
-            back_high = table_ref[512:640, columns]
-            return (
-                dot_nn(back_high, ch_ref[columns, :])
-                + dot_nn(back_high, cl_ref[columns, :])
-                + dot_nn(table_ref[640:768, columns], ch_ref[columns, :])
-            )
-
         for face in range(2, 6):
             coefficients(face, pair(dot_nn(fs_ref[face ^ 1], g_ref[face])))
         local = [pair(dot_nn(fs_ref[face ^ 1], g_ref[face])) for face in range(2)]
-        result = w_ref[:, 0:1] * value + conduct * f_ref[6 * FACE :, :] + backward(2, 6)
-        (after_moves, after_first)[step]()
+        result_ref[...] = (
+            w_ref[:, 0:1] * value_ref[...] + conduct * f_ref[6 * FACE :, :] + backward(2, 6)
+        )
+        return local
+
+    def ghost_part(step, local, copies):
+        parts = []
         for face in range(2):
             pl.when((has_left, has_right)[face])(copies[1 - face].wait_recv)
             high, low = split2(halo_recv[step, face])
             ghost = pair(dot_nn(jnp.concatenate([high, low], 0), gg_ref[face]))
-            coefficients(face, local[face] + ghost)
-        return result + backward(0, 2), copies
-
-    image, copies_one = operate(source, 0)
-    y_ref[...] = image
-    second_image, copies_two = operate(image, 1)
-
-    source = b_ref[...]
-    image = y_ref[...]
+            parts += coefficients(face, local[face] + ghost)
+        return parts
+
+    f_ref[...] = project(split2(with_conduct(b_ref[...])), slice(0, 6 * FACE + ROWS))
+    fb_ref[...] = f_ref[0 : 2 * FACE, :]
+    for side in range(2):
+        stack(side)
+    local = local_part(b_ref, y_ref)
+    faces_ahead = project(split2(with_conduct(y_ref[...])))
+    z_ref[...] = faces_ahead
+    whole_plane()
+    ghost_part(0, local, copies_one)
+    f_ref[0 : 2 * FACE, :] = z_ref[...] + expand(
+        table_ref[768:896, 0:128], table_ref[768:896, 128:256], slice(0, 2 * FACE)
+    )
+    for side in range(2):
+        stack(side)
+        halo_send[1, side] = pair(dot_nn(fs_ref[side], s_ref[side]))
+    copies_two = halo(1)
+    start_both(*copies_two)
+
+    y_ref[...] += backward(0, 2)
+    rest = slice(2 * FACE, 6 * FACE + ROWS)
+    f_ref[rest, :] = project(split2(with_conduct(y_ref[...])), rest)
+    local = local_part(y_ref, z_ref)
+
+    def summed(terms):
+        return jnp.sum(terms, axis=0, keepdims=True)
+
+    source, image, partial = b_ref[...], y_ref[...], z_ref[...]
+    early = [summed(source * source), summed(source * image), summed(image * image)]
+    late = [summed(source * partial), summed(image * partial)]
+    parts = jnp.concatenate(ghost_part(1, local, copies_two), 0) * w_ref[:, 1:2]
+    late = [late[0] + summed(fb_ref[...] * parts), late[1] + summed(f_ref[0 : 2 * FACE, :] * parts)]
     lane = lax.broadcasted_iota(jnp.int32, (1, 128), 1)
     row = jnp.zeros((1, 128), F32)
-    for index, terms in enumerate(
-        (source * source, source * image, image * image, source * second_image, image * second_image)
-    ):
-        row = row + jnp.where(lane == index, jnp.sum(terms, axis=(0, 1), keepdims=True), 0.0)
+    for index, terms in enumerate(early + late):
+        row = row + jnp.where(lane == index, jnp.sum(terms, axis=1, keepdims=True), 0.0)
 
     before_sums()
     sent = []
@@ -449,6 +493,8 @@
         row_send[phase] = row
         for i, peer in enumerate(peers):
             copy(row_send.at[phase], landing.at[i], ssem, rsem, peer).start()
+        if phase == 0:
+            z_ref[...] += backward(0, 2)
         every = copy(landing, landing, ssem, rsem, peers[0])
         every.wait_recv()
         terms = [row] + [landing[i] for i in range(len(peers))]
@@ -468,6 +514,7 @@
     alpha_next = norm_next / curvature
     first = alpha + alpha_next * grow
     second = alpha * alpha_next
+    source, image, second_image = b_ref[...], y_ref[...], z_ref[...]
     solution_out[...] = (first * source - second * image)[0:BLOCK]
     residual_out[...] = (source - first * image + second * second_image)[0:BLOCK]
     for one in sent:
@@ -506,6 +553,8 @@
             pltpu.VMEM((2, GHOST), jnp.int32),
             *[pltpu.VMEM(table.shape, table.dtype) for table in constants],
             pltpu.SemaphoreType.DMA((8,)),
+            pltpu.VMEM((ROWS, CELLS), F32),
+            pltpu.VMEM((ROWS, CELLS), F32),
             pltpu.VMEM((ROWS, CELLS), F32),
             pltpu.VMEM((ROWS, CELLS), F32),
             pltpu.VMEM((16, CELLS), F32),

time: 50.5 us -> 49.4 us (0.978)
  Pallas kernels: 49.7 us -> 48.6 us
    pallas_call x1, Pallas kernels: 48.9 us -> 47.8 us  [body(): call(right_side, conductivity[None], destination[None], neighbour, orient...]
where the time goes in v5:
time: 49.4 us; the launch traced here: 49.2 us
  Pallas kernels  48.6 us (98%)
  between operations  0.64 us (1%)
    pallas_call x1, Pallas kernels, body(): call(right_side, conductivity[None], destination[None], neighbour, orient...  47.8 us

profile of v5, /device:TPU:1, one launch (start us, length us, event | category | flops | bytes accessed | tf_op | source)
XLA Modules:
  0.0 49.2 jit_solution(17363665491449804073)
XLA Ops:
  0.6 47.8 %shard_map.95 = (f32[125,512]{1,0:T(8,128)S(1)}, f32[125,512]{1,0:T(8,128)S(1)}) custom-call(f32[125,512]{1,0:T(8,128)} %rs_hbm.1, f32[1,512]{1,0:T(1,128)} %bitcast.2, s32[1,512]{1,0:T(1,128)} %bitcast.3, s32[6,512]{1,0:T(8,128)} %nb_hbm.1, s32[6,512]{1,0:T(8,128)} %ori_hbm.1, s32[2,256]{1,0:T(2,128)} %sl_hbm.1, bf16[896,384]{1,0:T(8,128)(2,1)} %constant.4.clone.table_hbm, ...), custom_call_target="tpu_custom_call" | custom-call | tf_op jit(solution)/shard_map/pallas_call | solution.py:603
  48.4 0.8 %shard_map.96 = (f32[125,512]{1,0:T(8,128)}, f32[125,512]{1,0:T(8,128)}) custom-call(f32[125,512]{1,0:T(8,128)S(1)} %get-tuple-element.4.solution_ref, f32[125,512]{1,0:T(8,128)S(1)} %get-tuple-element.5.residual_ref), custom_call_target="tpu_custom_call" | custom-call | tf_op jit(solution)/shard_map/pallas_call | solution.py:607

commit v6 on v5

--- a/solution.py
+++ b/solution.py
@@ -17,6 +17,7 @@
 PENALTY = 80.0
 FACE = 64
 HALF = 32
+LISTED = HALF + 25
 ROWS = 128
 X_SIZE = 8
 MESH = pl.DeviceIdType.MESH
@@ -161,19 +162,25 @@
     solution_out, residual_out,
     rs_ref, cond_ref, dest_ref, nb_ref, ori_ref, sl_ref, table_ref, w_ref, load_sem,
     b_ref, y_ref, z_ref, fb_ref, tail_ref, x3_ref, q_ref, g_ref, gg_ref, s_ref, sign_ref, f_ref, fs_ref, ch_ref, cl_ref,
-    mig_send, mig_recv, halo_send, halo_recv, row_send, curve_recv, group_recv,
-    mig_ssem, mig_rsem, halo_ssem, halo_rsem, curve_ssem, curve_rsem, group_ssem, group_rsem, one_sem, two_sem, plane_sem,
+    mig_send, mig_recv, far_recv, halo_send, halo_recv, row_send, curve_recv, group_recv,
+    mig_ssem, mig_rsem, far_ssem, far_rsem, halo_ssem, halo_rsem, curve_ssem, curve_rsem, group_ssem, group_rsem, one_sem, two_sem, plane_sem,
 ):
     curve = lax.axis_index("curve")
     group = lax.axis_index("group")
     me = curve * n_group + group
     total = n_curve * n_group
     has_left, has_right = me > 0, me < total - 1
+    edge_left, edge_right = (group == 0) & has_left, (group == n_group - 1) & has_right
+    plain_left = has_left & jnp.logical_not(edge_left)
+    plain_right = has_right & jnp.logical_not(edge_right)
+    far_left = (group == 1) & (curve > 0)
+    far_right = (group == n_group - 2) & (curve < n_curve - 1)
 
     def device(rank):
         return (rank // n_group, lax.rem(rank, n_group))
 
     left, right = device(lax.rem(me + total - 1, total)), device(lax.rem(me + 1, total))
+    left_two, right_two = device(lax.rem(me + total - 2, total)), device(lax.rem(me + 2, total))
     z_size = n_group // x_size
     x_pos = lax.rem(group, x_size)
     z_pos = group // x_size
@@ -236,6 +243,14 @@
     @pl.when(has_right)
     def _():
         signal(barrier, right)
+
+    @pl.when(edge_left)
+    def _():
+        signal(barrier, left_two)
+
+    @pl.when(edge_right)
+    def _():
+        signal(barrier, right_two)
 
     loads = {}
     for i, (name, source, sink) in enumerate(
@@ -291,7 +306,8 @@
     packed = dot_nt(onehot(place, 2 * MOVE), x3_ref[...])
     mig_send[...] = packed[:, 0:ROWS] + packed[:, ROWS : 2 * ROWS] + packed[:, 2 * ROWS :]
 
-    pl.semaphore_wait(barrier, len(near_peers) + has_left.astype(jnp.int32) + has_right.astype(jnp.int32))
+    greeted = [has_left, has_right, far_left, far_right]
+    pl.semaphore_wait(barrier, len(near_peers) + sum(one.astype(jnp.int32) for one in greeted))
 
     def copy(source, sink, ssem, rsem, peer):
         return pltpu.make_async_remote_copy(
@@ -309,6 +325,10 @@
         mig_send.at[pl.ds(MOVE, MOVE)], mig_recv.at[pl.ds(0, MOVE)], mig_ssem.at[1], mig_rsem.at[1], right
     )
     start_both(to_left, to_right)
+    to_far_left = copy(mig_send.at[pl.ds(0, MOVE)], far_recv, far_ssem.at[0], far_rsem, left_two)
+    to_far_right = copy(mig_send.at[pl.ds(MOVE, MOVE)], far_recv, far_ssem.at[1], far_rsem, right_two)
+    pl.when(far_left)(to_far_left.start)
+    pl.when(far_right)(to_far_right.start)
     spread(1, one_sem)
     loads["nb"].wait()
     loads["sl"].wait()
@@ -351,6 +371,10 @@
     for side in range(2):
         stack(side)
         halo_send[0, side] = pair(dot_nn(fs_ref[side], s_ref[side]))
+        halo_send[0, side, LISTED : LISTED + 1, :] = sl_ref[side : side + 1, :].astype(F32)
+    copies_one = halo(0)
+    pl.when(edge_left)(copies_one[0].start)
+    pl.when(edge_right)(copies_one[1].start)
     mode = lax.broadcasted_iota(jnp.int32, (HALF, CELLS), 0)
     odd_first = jnp.where((mode >= 15) & (mode < 25), 2.0, 0.0)
     second = functools.reduce(jnp.logical_or, [mode == 5 * i + j for i in range(5) for j in (3, 4)])
@@ -374,14 +398,23 @@
     pl.when(has_right)(to_left.wait_recv)
 
     arrived = mig_recv[...].T
-    slot_in = mig_recv[:, BLOCK + 1 : BLOCK + 2].astype(jnp.int32) - 1
     faces = project(split2(arrived))
-    for side in range(2):
-        listed = jnp.where(slot_in == sl_ref[side : side + 1, :], 1.0, 0.0).astype(BF16)
-        parts = jnp.concatenate(split2(faces[side * FACE : (side + 1) * FACE]), 0)
-        halo_send[0, side] += pair(dot_nn(parts, listed))
-    copies_one = halo(0)
-    start_both(*copies_one)
+
+    def place_faces(faces, records, listed):
+        slots = records[:, BLOCK + 1 : BLOCK + 2].astype(jnp.int32) - 1
+        chosen = jnp.where(slots == listed, 1.0, 0.0).astype(BF16)
+        return pair(dot_nn(jnp.concatenate(split2(faces), 0), chosen))
+
+    came = mig_recv[...]
+    for side, plain in ((0, plain_left), (1, plain_right)):
+        more = place_faces(faces[side * FACE : (side + 1) * FACE], came, sl_ref[side : side + 1, :])
+
+        @pl.when(plain)
+        def _():
+            halo_send[0, side] += more
+
+    pl.when(plain_left)(copies_one[0].start)
+    pl.when(plain_right)(copies_one[1].start)
 
     place_in = arrived[BLOCK + 1 : BLOCK + 2, :].astype(jnp.int32) - 1
     for start in range(0, CELLS, 128):
@@ -437,10 +470,23 @@
         )
         return local
 
+    def complete(face, incoming):
+        incoming.wait_recv()
+        to_far_left.wait_recv()
+        records = jnp.concatenate([mig_send[face * MOVE : (face + 1) * MOVE, :], far_recv[...]], 0)
+        other = 1 - face
+        faces = project(split2(records.T), slice(other * FACE, (other + 1) * FACE))
+        listed = halo_recv[0, face, LISTED : LISTED + 1, :].astype(jnp.int32)
+        halo_recv[0, face] += place_faces(faces, records, listed)
+
     def ghost_part(step, local, copies):
         parts = []
         for face in range(2):
-            pl.when((has_left, has_right)[face])(copies[1 - face].wait_recv)
+            if step == 0:
+                pl.when((plain_left, plain_right)[face])(copies[1 - face].wait_recv)
+                pl.when((edge_left, edge_right)[face])(functools.partial(complete, face, copies[1 - face]))
+            else:
+                pl.when((has_left, has_right)[face])(copies[1 - face].wait_recv)
             high, low = split2(halo_recv[step, face])
             ghost = pair(dot_nn(jnp.concatenate([high, low], 0), gg_ref[face]))
             parts += coefficients(face, local[face] + ghost)
@@ -519,6 +565,8 @@
     residual_out[...] = (source - first * image + second * second_image)[0:BLOCK]
     for one in sent:
         one.wait_send()
+    pl.when(far_left)(to_far_left.wait_send)
+    pl.when(far_right)(to_far_right.wait_send)
     for one_left, one_right in ((to_left, to_right), copies_one, copies_two):
         pl.when(has_left)(one_left.wait_send)
         pl.when(has_right)(one_right.wait_send)
@@ -570,6 +618,7 @@
             pltpu.VMEM((6 * FACE, CELLS), BF16),
             pltpu.VMEM((2 * MOVE, ROWS), F32),
             pltpu.VMEM((2 * MOVE, ROWS), F32),
+            pltpu.VMEM((MOVE, ROWS), F32),
             pltpu.VMEM((2, 2, FACE, GHOST), F32),
             pltpu.VMEM((2, 2, FACE, GHOST), F32),
             pltpu.VMEM((2, 1, 128), F32),
@@ -577,6 +626,8 @@
             pltpu.VMEM((n_group - 1, 1, 128), F32),
             pltpu.SemaphoreType.DMA((2,)),
             pltpu.SemaphoreType.DMA((2,)),
+            pltpu.SemaphoreType.DMA((2,)),
+            pltpu.SemaphoreType.DMA,
             pltpu.SemaphoreType.DMA((2, 2)),
             pltpu.SemaphoreType.DMA((2, 2)),
             pltpu.SemaphoreType.DMA,

time: 49.4 us -> 47.4 us (0.960)
  Pallas kernels: 48.6 us -> 46.6 us
    pallas_call x1, Pallas kernels: 47.8 us -> 45.8 us  [body(): call(right_side, conductivity[None], destination[None], neighbour, orient...]
where the time goes in v6:
time: 47.4 us; the launch traced here: 47.2 us
  Pallas kernels  46.6 us (98%)
  between operations  0.64 us (1%)
    pallas_call x1, Pallas kernels, body(): call(right_side, conductivity[None], destination[None], neighbour, orient...  45.8 us

profile of v6, /device:TPU:1, one launch (start us, length us, event | category | flops | bytes accessed | tf_op | source)
XLA Modules:
  0.0 47.2 jit_solution(7496014210693888234)
XLA Ops:
  0.6 45.8 %shard_map.95 = (f32[125,512]{1,0:T(8,128)S(1)}, f32[125,512]{1,0:T(8,128)S(1)}) custom-call(f32[125,512]{1,0:T(8,128)} %rs_hbm.1, f32[1,512]{1,0:T(1,128)} %bitcast.2, s32[1,512]{1,0:T(1,128)} %bitcast.3, s32[6,512]{1,0:T(8,128)} %nb_hbm.1, s32[6,512]{1,0:T(8,128)} %ori_hbm.1, s32[2,256]{1,0:T(2,128)} %sl_hbm.1, bf16[896,384]{1,0:T(8,128)(2,1)} %constant.4.clone.table_hbm, ...), custom_call_target="tpu_custom_call" | custom-call | tf_op jit(solution)/shard_map/pallas_call | solution.py:654
  46.4 0.8 %shard_map.96 = (f32[125,512]{1,0:T(8,128)}, f32[125,512]{1,0:T(8,128)}) custom-call(f32[125,512]{1,0:T(8,128)S(1)} %get-tuple-element.4.solution_ref, f32[125,512]{1,0:T(8,128)S(1)} %get-tuple-element.5.residual_ref), custom_call_target="tpu_custom_call" | custom-call | tf_op jit(solution)/shard_map/pallas_call | solution.py:658

commit v7 on v6

--- a/solution.py
+++ b/solution.py
@@ -480,8 +480,8 @@
         halo_recv[0, face] += place_faces(faces, records, listed)
 
     def ghost_part(step, local, copies):
-        parts = []
-        for face in range(2):
+        parts = [(), ()]
+        for face in ((0, 1), (1, 0))[step]:
             if step == 0:
                 pl.when((plain_left, plain_right)[face])(copies[1 - face].wait_recv)
                 pl.when((edge_left, edge_right)[face])(functools.partial(complete, face, copies[1 - face]))
@@ -489,8 +489,8 @@
                 pl.when((has_left, has_right)[face])(copies[1 - face].wait_recv)
             high, low = split2(halo_recv[step, face])
             ghost = pair(dot_nn(jnp.concatenate([high, low], 0), gg_ref[face]))
-            parts += coefficients(face, local[face] + ghost)
-        return parts
+            parts[face] = coefficients(face, local[face] + ghost)
+        return parts[0] + parts[1]
 
     f_ref[...] = project(split2(with_conduct(b_ref[...])), slice(0, 6 * FACE + ROWS))
     fb_ref[...] = f_ref[0 : 2 * FACE, :]
@@ -504,11 +504,11 @@
     f_ref[0 : 2 * FACE, :] = z_ref[...] + expand(
         table_ref[768:896, 0:128], table_ref[768:896, 128:256], slice(0, 2 * FACE)
     )
-    for side in range(2):
+    copies_two = halo(1)
+    for side, there in ((1, has_right), (0, has_left)):
         stack(side)
         halo_send[1, side] = pair(dot_nn(fs_ref[side], s_ref[side]))
-    copies_two = halo(1)
-    start_both(*copies_two)
+        pl.when(there)(copies_two[side].start)
 
     y_ref[...] += backward(0, 2)
     rest = slice(2 * FACE, 6 * FACE + ROWS)

time: 47.4 us -> 47.2 us (level)
  no operation moved by 1% of the time
where the time goes in v7:
time: 47.2 us; the launch traced here: 47 us
  Pallas kernels  46.4 us (98%)
  between operations  0.64 us (1%)
    pallas_call x1, Pallas kernels, body(): call(right_side, conductivity[None], destination[None], neighbour, orient...  45.6 us

profile of v7, /device:TPU:1, one launch (start us, length us, event | category | flops | bytes accessed | tf_op | source)
XLA Modules:
  0.0 47.0 jit_solution(6920379710292715094)
XLA Ops:
  0.6 45.6 %shard_map.95 = (f32[125,512]{1,0:T(8,128)S(1)}, f32[125,512]{1,0:T(8,128)S(1)}) custom-call(f32[125,512]{1,0:T(8,128)} %rs_hbm.1, f32[1,512]{1,0:T(1,128)} %bitcast.2, s32[1,512]{1,0:T(1,128)} %bitcast.3, s32[6,512]{1,0:T(8,128)} %nb_hbm.1, s32[6,512]{1,0:T(8,128)} %ori_hbm.1, s32[2,256]{1,0:T(2,128)} %sl_hbm.1, bf16[896,384]{1,0:T(8,128)(2,1)} %constant.4.clone.table_hbm, ...), custom_call_target="tpu_custom_call" | custom-call | tf_op jit(solution)/shard_map/pallas_call | solution.py:654
  46.2 0.8 %shard_map.96 = (f32[125,512]{1,0:T(8,128)}, f32[125,512]{1,0:T(8,128)}) custom-call(f32[125,512]{1,0:T(8,128)S(1)} %get-tuple-element.4.solution_ref, f32[125,512]{1,0:T(8,128)S(1)} %get-tuple-element.5.residual_ref), custom_call_target="tpu_custom_call" | custom-call | tf_op jit(solution)/shard_map/pallas_call | solution.py:658
